TPU v7x, 128 devices: a whole 4x4x4 slice. The times are simulated.
128 devices in a mesh: dp: 8 (over y_lo, x), tensor: 16 (over y_hi, z, core).
Axes of the slice: x: 4, y: 4 (y_hi: 2, y_lo: 2; y = y_hi * 2 + y_lo), z: 4, core: 2. Of those that a mesh axis runs over, the one named last changes fastest.
Arguments:
- saved_input: bfloat16 [1024, 8192], P(('dp', 'tensor')), may hold values from -8 to 8
- keep_bits: int32 [1024, 448], P(('dp', 'tensor')), may hold values from -2147483648 to 2147483646, as said below
- norm_gain: bfloat16 [8192], P('dp'), may hold values from 0.099609375 to 1.8984375
- gate_weight: bfloat16 [8192, 14336], P('dp', 'tensor'), may hold values from -0.0625 to 0.0625
- up_weight: bfloat16 [8192, 14336], P('dp', 'tensor'), may hold values from -0.0625 to 0.0625
- down_weight: bfloat16 [14336, 8192], P('tensor', 'dp'), may hold values from -0.046875 to 0.046875
Outputs:
- layer_out: bfloat16 [1024, 8192], P('tensor', 'dp')
- row_check: float32 [1024], P('tensor')
Inputs may be any that keep to these rules, and one draw needn't show every extreme that they name: `keep_bits`: bit k of word w of a token is the keep bit of hidden unit 32 w + k.
All inputs are finite; a program needn't handle non-finite values.
Results may differ from a plain program's by a relative error of at most 0.017.
Values may be sent and summed in bfloat16 or wider, within the bound.
A program may use at most 64 MiB of HBM per device.

v0:
```python
import jax
import jax.numpy as jnp
from jax import lax
from jax.sharding import Mesh
from jax.sharding import PartitionSpec as P

D = 8192
TENSOR = ("tensor_0", "tensor_1", "tensor_2")
DP_TENSOR = ("dp", "tensor_0", "tensor_1", "tensor_2")


def sent_to_all(value, axis):
    length = lax.axis_size(axis)
    return lax.all_to_all(
        jnp.broadcast_to(value[None], (length, *value.shape)), axis, 0, 0, tiled=True
    )


def laid_out(parts, dim):
    lengths = list(parts.shape[1:])
    lengths[dim] *= parts.shape[0]
    return jnp.moveaxis(parts, 0, dim).reshape(lengths)


def whole_of(value, axes, dim):
    far, near = axes
    leading = sent_to_all(value, far)
    parts = jnp.swapaxes(sent_to_all(leading, near), 0, 1)
    return laid_out(parts.reshape(-1, *value.shape), dim)


def over_copies(value, axis):
    everything = sent_to_all(value, axis)
    return jnp.sum(everything, axis=0)


def gathered_copies(value, axis, dim):
    return laid_out(sent_to_all(value, axis), dim)


def in_blocks(value, dim, length):
    before, after = (value.shape[:dim], value.shape[dim + 1 :])
    return jnp.moveaxis(value.reshape(*before, length, -1, *after), dim, 0)


def sum_at_owner(value, axis, dim):
    length = lax.axis_size(axis)
    parts = lax.all_to_all(in_blocks(value, dim, length), axis, 0, 0, tiled=True)
    return jnp.sum(parts.astype(jnp.float32), axis=0)


def sum_in_two_steps(value, axes, dim):
    far, near = axes
    parts = in_blocks(value, dim, lax.axis_size(far))
    nearer = sum_at_owner(parts, near, dim + 1)
    arrived = lax.all_to_all(
        nearer.astype(jnp.bfloat16), far, split_axis=0, concat_axis=0, tiled=True
    )
    return arrived.astype(jnp.float32).sum(axis=0)


def on_device(saved_input, keep_bits, norm_gain, gate_weight, up_weight, down_weight):
    tensor_width = lax.axis_size(TENSOR)
    dp_width = lax.axis_size("dp")
    unit_words = lax.all_to_all(keep_bits, TENSOR, split_axis=1, concat_axis=0, tiled=True)
    shifts = jnp.arange(32, dtype=jnp.int32)
    keep_mask = jnp.bitwise_and(jnp.right_shift(unit_words[:, :, None], shifts[None, None, :]), 1)
    keep_mask = keep_mask.reshape(unit_words.shape[0], -1)
    keep_scale = 2.0 * keep_mask.astype(jnp.float32)
    width_units = gate_weight.shape[1]
    columns = lax.all_to_all(saved_input, "dp", split_axis=1, concat_axis=0, tiled=True)
    collected = whole_of(columns, (("tensor_0", "tensor_1"), "tensor_2"), 0)
    per_device = saved_input.shape[0]
    collected = collected.reshape(tensor_width, dp_width, per_device, collected.shape[1])
    collected = collected.transpose(1, 0, 2, 3).reshape(-1, collected.shape[3])
    widened = collected.astype(jnp.float32)
    squares = over_copies(jnp.sum(widened * widened, axis=1), "dp")
    inv_rms = lax.rsqrt(squares / D + 1e-05)
    normed = (widened * inv_rms[:, None] * norm_gain.astype(jnp.float32)[None, :]).astype(
        jnp.bfloat16
    )
    gate_part = jnp.dot(normed, gate_weight, preferred_element_type=jnp.float32)
    up_part = jnp.dot(normed, up_weight, preferred_element_type=jnp.float32)
    projected = lax.psum_scatter(
        jnp.concatenate((gate_part, up_part), axis=1).astype(jnp.bfloat16),
        "dp",
        scatter_dimension=0,
        tiled=True,
    ).astype(jnp.float32)
    gate_sum = projected[:, :width_units]
    up_sum = projected[:, width_units:]
    hidden = (jax.nn.silu(gate_sum) * up_sum * keep_scale).astype(jnp.bfloat16)
    partial_value = jnp.dot(
        gathered_copies(hidden, "dp", 0), down_weight, preferred_element_type=jnp.float32
    )
    mlp_sum = sum_in_two_steps(
        partial_value.astype(jnp.bfloat16), (("tensor_0", "tensor_1"), "tensor_2"), 0
    )
    out_rows = mlp_sum.shape[0]
    first_row = lax.axis_index(TENSOR) * out_rows
    residual = lax.dynamic_slice_in_dim(collected, first_row, out_rows, 0)
    layer_out = (residual.astype(jnp.float32) + mlp_sum).astype(jnp.bfloat16)
    widened_out = layer_out.astype(jnp.float32)
    row_check = over_copies(jnp.sum(widened_out * widened_out, axis=1), "dp") / D
    return (layer_out, row_check)


def solution(mesh):
    torus = Mesh(
        mesh.devices.reshape(mesh.shape["dp"], 2, 4, 2), ("dp", "tensor_0", "tensor_1", "tensor_2")
    )
    return jax.shard_map(
        on_device,
        mesh=torus,
        in_specs=(
            P(DP_TENSOR, None),
            P(DP_TENSOR, None),
            P("dp"),
            P("dp", TENSOR),
            P("dp", TENSOR),
            P(TENSOR, "dp"),
        ),
        out_specs=(P(TENSOR, "dp"), P(TENSOR)),
        check_vma=False,
    )
```

profile of v0, /device:TPU:1, one launch (start us, length us, event | category | flops | bytes accessed | tf_op | source)
XLA Modules:
  0.0 198.2 jit_solution(10740757617195257877)
XLA Ops:
  7.2 0.0 copy-start
  7.2 11.4 %all_to_all.69 = bf16[8,8,1024]{2,0,1:T(8,128)(2,1)S(1)} all-to-all(bf16[8,8,1024]{2,0,1:T(8,128)(2,1)} %bitcast.50), channel_id=1, replica_groups=mesh['dp'=8,'tensor_0'=2,'tensor_1'=4,'tensor_2'=2] {'dp'}, dimensions={1} | all-to-all | bytes 262144 | tf_op jit(solution)/shard_map/all_to_all | solution.py:71
  18.6 0.1 broadcast_in_dim.15
  18.8 21.4 %all_to_all.70 = bf16[8,64,1024]{2,1,0:T(8,128)(2,1)S(1)} all-to-all(bf16[8,64,1024]{2,1,0:T(8,128)(2,1)S(1)} %broadcast_in_dim.15), channel_id=1, replica_groups=mesh['dp'=8,'tensor_0'=2,'tensor_1'=4,'tensor_2'=2] {'tensor_0','tensor_1'}, dimensions={0} | all-to-all | bytes 2097152 | tf_op jit(solution)/shard_map/all_to_all | solution.py:14
  40.2 0.3 broadcast_in_dim.16
  40.4 8.9 %all_to_all.71 = bf16[2,8,64,1024]{3,2,1,0:T(8,128)(2,1)S(1)} all-to-all(bf16[2,8,64,1024]{3,2,1,0:T(8,128)(2,1)S(1)} %broadcast_in_dim.16), channel_id=1, replica_groups=mesh['dp'=8,'tensor_0'=2,'tensor_1'=4,'tensor_2'=2] {'tensor_2'}, dimensions={0} | all-to-all | bytes 4194304 | tf_op jit(solution)/shard_map/all_to_all | solution.py:14
  49.3 0.2 copy.30
  49.6 0.0 copy-start.4
  49.6 1.3 copy-done.1
  50.9 0.5 multiply_reduce_fusion
  51.4 0.1 broadcast_in_dim.17
  51.5 0.6 broadcast_in_dim.18
  52.1 3.3 %all-to-all-start.3 = ((f32[8,1,1024]{2,1,0:T(1,128)}), f32[8,1,1024]{2,1,0:T(1,128)S(1)}, u32[]{:S(2)}, u32[]{:S(2)}) async-start(f32[8,1,1024]{2,1,0:T(1,128)} %broadcast_in_dim.18), calls=%async_computation.3 | async-start | bytes 65536 | tf_op jit(solution)/shard_map/all_to_all | solution.py:14
  55.5 0.0 reduce-scatter.4.cloned.1.call-start
  55.6 3.2 %copy.31 = bf16[8,16,8,1024]{3,2,1,0:T(8,128)(2,1)} copy(bf16[8,16,8,1024]{3,2,0,1:T(8,128)(2,1)} %bitcast.41) | data formatting | bytes 4194304 | tf_op jit(solution)/shard_map/transpose | solution.py:75
  58.8 1.8 all-to-all-done.3
  60.6 4.6 %convolution_convert_fusion.1 = bf16[1024,896]{0,1:T(8,128)(2,1)S(1)} fusion(bf16[1024,896]{1,0:T(8,128)(2,1)} %param.10, bf16[1024,1024]{1,0:T(8,128)(2,1)} %bitcast.43, f32[1024]{0:T(1024)S(1)} %convert_element_type.42, f32[1024]{0:T(1024)S(1)} %add_rsqrt_fusion), kind=kOutput, calls=%fused_computation.6 | convolution fusion | flops 1884160000 | bytes 5775360 | tf_op jit(solution)/shard_map/dot_general | solution.py:83
  65.2 2.3 %convolution_convert_fusion.2 = bf16[1024,896]{0,1:T(8,128)(2,1)S(1)} fusion(bf16[1024,896]{1,0:T(8,128)(2,1)S(1)} %copy-done.5, bf16[1024,1024]{1,0:T(8,128)(2,1)S(1)} %bitcast.45, f32[1024]{0:T(1024)S(1)} %convert_element_type.42, f32[1024]{0:T(1024)S(1)} %add_rsqrt_fusion), kind=kOutput, calls=%fused_computation.7 | convolution fusion | flops 1884160000 | bytes 5775360 | tf_op jit(solution)/shard_map/dot_general | solution.py:82
  67.5 2.2 %pad_maximum_fusion = bf16[1024,1792]{0,1:T(8,128)(2,1)} fusion(bf16[1024,896]{0,1:T(8,128)(2,1)S(1)} %convolution_convert_fusion.1, bf16[1024,896]{0,1:T(8,128)(2,1)S(1)} %convolution_convert_fusion.2), kind=kLoop, calls=%fused_computation.2 | loop fusion | flops 7340032 | bytes 7340032 | tf_op jit(solution)/shard_map/concatenate | solution.py:85
  69.7 6.0 %copy.39 = bf16[1024,1792]{1,0:T(8,128)(2,1)} copy(bf16[1024,1792]{0,1:T(8,128)(2,1)} %pad_maximum_fusion) | data formatting | bytes 7340032
  75.7 0.0 reduce-scatter.4.cloned.1.call-update
  75.7 0.7 copy-done.3
  76.4 0.1 all_to_all.53
  76.6 0.7 reshape.51
  77.3 4.8 %all-to-all-start.4 = ((s32[16,1,224]{2,1,0:T(1,128)}), s32[16,1,224]{2,1,0:T(1,128)S(1)}, u32[]{:S(2)}, u32[]{:S(2)}) async-start(s32[16,1,224]{2,1,0:T(1,128)} %reshape.51), calls=%async_computation.4 | async-start | bytes 32768 | tf_op jit(solution)/shard_map/all_to_all | solution.py:65
  82.1 0.1 shift_right_arithmetic.26
  82.2 7.5 %all-to-all-done.4 = s32[16,1,224]{2,1,0:T(1,128)S(1)} async-done(((s32[16,1,224]{2,1,0:T(1,128)}), s32[16,1,224]{2,1,0:T(1,128)S(1)}, u32[]{:S(2)}, u32[]{:S(2)}) %all-to-all-start.4) | async-done | bytes 14368 | tf_op jit(solution)/shard_map/all_to_all | solution.py:65
  89.7 0.5 broadcast.25
  90.2 0.7 reduce.4
  90.9 0.1 reshape.52
  91.0 0.1 copy.35
  91.1 27.7 %reduce-scatter.4.cloned.1.call-done = bf16[128,1792]{1,0:T(8,128)(2,1)} async-done(((bf16[1024,1792]{1,0:T(8,128)(2,1)}), bf16[128,1792]{1,0:T(8,128)(2,1)}) %reduce-scatter.4.cloned.1.call-update) | async-done | bytes 458768
  118.8 1.3 copy.40
  120.0 0.1 convert_element_type.44
  120.1 0.2 fusion.1
  120.3 0.2 copy.36
  120.5 0.2 broadcast_in_dim.19
  120.7 24.6 %all_to_all.72 = bf16[8,128,896]{2,1,0:T(8,128)(2,1)S(1)} all-to-all(bf16[8,128,896]{2,1,0:T(8,128)(2,1)S(1)} %broadcast_in_dim.19), channel_id=1, replica_groups=mesh['dp'=8,'tensor_0'=2,'tensor_1'=4,'tensor_2'=2] {'dp'}, dimensions={0} | all-to-all | bytes 3670016 | tf_op jit(solution)/shard_map/all_to_all | solution.py:14
  145.4 2.3 %convolution_convert_fusion = bf16[1024,1024]{1,0:T(8,128)(2,1)S(1)} fusion(bf16[1024,896]{1,0:T(8,128)(2,1)S(1)} %bitcast.47, bf16[896,1024]{1,0:T(8,128)(2,1)S(1)} %copy-done), kind=kOutput, calls=%fused_computation.5 | convolution fusion | flops 1880096768 | bytes 5767168 | tf_op jit(solution)/shard_map/dot_general | solution.py:93
  147.7 0.2 copy.44
  147.9 9.4 %all_to_all.73 = bf16[2,8,64,1024]{3,2,1,0:T(8,128)(2,1)} all-to-all(bf16[2,8,64,1024]{3,2,1,0:T(8,128)(2,1)S(1)} %bitcast.42), channel_id=1, replica_groups=mesh['dp'=8,'tensor_0'=2,'tensor_1'=4,'tensor_2'=2] {'tensor_2'}, dimensions={0} | all-to-all | bytes 4194304 | tf_op jit(solution)/shard_map/all_to_all | solution.py:48
  157.4 3.4 %reduce_sum.59 = bf16[8,64,1024]{2,1,0:T(8,128)(2,1)} reduce(bf16[2,8,64,1024]{3,2,1,0:T(8,128)(2,1)} %all_to_all.73, bf16[]{:T(256)} %constant.38.clone.1), dimensions={0}, to_apply=%region_3.4 | reduce | flops 524288 | bytes 3145730 | tf_op jit(solution)/shard_map/reduce_sum | solution.py:49
  160.7 6.3 %all-to-all-start.7 = ((bf16[8,64,1024]{2,1,0:T(8,128)(2,1)}), bf16[8,64,1024]{2,1,0:T(8,128)(2,1)S(1)}, u32[]{:S(2)}, u32[]{:S(2)}) async-start(bf16[8,64,1024]{2,1,0:T(8,128)(2,1)} %reduce_sum.59), calls=%async_computation.7 | async-start | bytes 2097152 | tf_op jit(solution)/shard_map/all_to_all | solution.py:56
  167.0 14.5 %all-to-all-done.7 = bf16[8,64,1024]{2,1,0:T(8,128)(2,1)S(1)} async-done(((bf16[8,64,1024]{2,1,0:T(8,128)(2,1)}), bf16[8,64,1024]{2,1,0:T(8,128)(2,1)S(1)}, u32[]{:S(2)}, u32[]{:S(2)}) %all-to-all-start.7) | async-done | bytes 1048608 | tf_op jit(solution)/shard_map/all_to_all | solution.py:56
  181.5 0.2 convert_reduce_fusion
  181.7 1.7 multiply_reduce_fusion.1
  183.4 7.4 %all_to_all.74 = f32[8,1,64]{2,1,0:T(1,128)S(1)} all-to-all(f32[8,1,64]{2,1,0:T(1,128)S(1)} %broadcast_in_dim.20), channel_id=1, replica_groups=mesh['dp'=8,'tensor_0'=2,'tensor_1'=4,'tensor_2'=2] {'dp'}, dimensions={0} | all-to-all | bytes 4096 | tf_op jit(solution)/shard_map/all_to_all | solution.py:14
  190.8 0.5 broadcast_multiply_fusion
  (17 shorter events, 0.1 us)
Async XLA Ops:
  7.2 138.2 %copy-start = (bf16[896,1024]{1,0:T(8,128)(2,1)S(1)}, bf16[896,1024]{1,0:T(8,128)(2,1)}, u32[]{:S(2)}) copy-start(bf16[896,1024]{1,0:T(8,128)(2,1)} %param.11) | copy-start | bytes 5505028
  49.6 1.4 copy-start.1
  49.6 6.0 %copy-start.4 = (bf16[1024]{0:T(1024)(128)(2,1)S(1)}, bf16[1024]{0:T(1024)(128)(2,1)}, u32[]{:S(2)}) copy-start(bf16[1024]{0:T(1024)(128)(2,1)} %param.8) | copy-start | bytes 6148
  52.1 8.4 %all-to-all-start.3 = ((f32[8,1,1024]{2,1,0:T(1,128)}), f32[8,1,1024]{2,1,0:T(1,128)S(1)}, u32[]{:S(2)}, u32[]{:S(2)}) async-start(f32[8,1,1024]{2,1,0:T(1,128)} %broadcast_in_dim.18), calls=%async_computation.3 | async-start | bytes 65536 | tf_op jit(solution)/shard_map/all_to_all | solution.py:14
  55.5 63.3 %reduce-scatter.4.cloned.1.call-start = ((), (), s32[]{:S(2)}) async-start(), calls=%async_computation.10 | async-start | bytes 4128768
  60.6 4.6 %copy-start.2 = (bf16[8,16,8,1024]{3,2,1,0:T(8,128)(2,1)S(1)}, bf16[8,16,8,1024]{3,2,1,0:T(8,128)(2,1)}, u32[]{:S(2)}) copy-start(bf16[8,16,8,1024]{3,2,1,0:T(8,128)(2,1)} %copy.31) | copy-start | bytes 6291460
  60.6 4.6 %copy-start.5 = (bf16[1024,896]{1,0:T(8,128)(2,1)S(1)}, bf16[1024,896]{1,0:T(8,128)(2,1)}, u32[]{:S(2)}) copy-start(bf16[1024,896]{1,0:T(8,128)(2,1)} %param.9) | copy-start | bytes 5505028
  75.7 0.7 copy-start.3
  77.3 12.4 %all-to-all-start.4 = ((s32[16,1,224]{2,1,0:T(1,128)}), s32[16,1,224]{2,1,0:T(1,128)S(1)}, u32[]{:S(2)}, u32[]{:S(2)}) async-start(s32[16,1,224]{2,1,0:T(1,128)} %reshape.51), calls=%async_computation.4 | async-start | bytes 32768 | tf_op jit(solution)/shard_map/all_to_all | solution.py:65
  160.7 20.8 %all-to-all-start.7 = ((bf16[8,64,1024]{2,1,0:T(8,128)(2,1)}), bf16[8,64,1024]{2,1,0:T(8,128)(2,1)S(1)}, u32[]{:S(2)}, u32[]{:S(2)}) async-start(bf16[8,64,1024]{2,1,0:T(8,128)(2,1)} %reduce_sum.59), calls=%async_computation.7 | async-start | bytes 2097152 | tf_op jit(solution)/shard_map/all_to_all | solution.py:56
Sparse Core Ops, SparseCore 0:
  75.9 42.8 reduce-scatter.3
where the time goes:
time: 201 us; the launch traced here: 198 us
  blocking collectives  83.2 us (41%)
  waiting for transfers between devices  51.5 us (26%)
  local copies, waits for them, and re-layouts  16 us (8%)
  starting transfers between devices  14.5 us (7%)
  between operations  14.3 us (7%)
  other arithmetic  9.45 us (5%)
  matrix products  9.25 us (5%)
    all_to_all x4, blocking collectives, sent_to_all(): lax.all_to_all(jnp.broadcast_to(value[None], (length, *value.shape)), axi...  62.3 us
    unnamed x2, waiting for transfers between devices  27.7 us
    all_to_all x1, waiting for transfers between devices, sum_in_two_steps(): lax.all_to_all(nearer.astype(jnp.bfloat16), far, split_axis=0, concat_axi...  14.5 us
    all_to_all x1, blocking collectives, on_device(): lax.all_to_all(saved_input, 'dp', split_axis=1, concat_axis=0, tiled=True)  11.4 us
    unnamed x16, local copies, waits for them, and re-layouts  10.1 us
    all_to_all x1, blocking collectives, sum_at_owner(): lax.all_to_all(in_blocks(value, dim, length), axis, 0, 0, tiled=True)  9.44 us
    all_to_all x1, waiting for transfers between devices, on_device(): lax.all_to_all(keep_bits, TENSOR, split_axis=1, concat_axis=0, tiled=True)  7.54 us
    all_to_all x1, starting transfers between devices, sum_in_two_steps(): lax.all_to_all(nearer.astype(jnp.bfloat16), far, split_axis=0, concat_axi...  6.26 us
  transfers between devices with their start and end apart: 4, of which 4 were waited for; matrix products, arithmetic and copies ran while one was open for 3% of the time, Pallas kernels for 0%

commit v1 on v0

v1 whole, which is shorter than its diff:
```python
import jax
import jax.numpy as jnp
from jax import lax
from jax.experimental import pallas as pl
from jax.experimental.pallas import tpu as pltpu
from jax.sharding import PartitionSpec as P

D = 8192
DS = 1024
FU = 896
MESH = pl.DeviceIdType.MESH
F32 = jnp.float32
BF16 = jnp.bfloat16
NX, NY, NH, NZ = 4, 2, 2, 4
OFFSETS = (0, 1, 3, 2)


def kernel(
    x_ref,
    kb_ref,
    gain_ref,
    wg_ref,
    wu_ref,
    wd_ref,
    out_ref,
    rc_ref,
    w,
    wd,
    spread,
    xb,
    xn,
    part,
    relay,
    rx,
    ysend,
    yrecv,
    hid,
    osum,
    orecv,
    fsend,
    frecv,
    csend,
    crecv,
    w_sem,
    l_sem,
    a_send,
    a_recv,
    x_send,
    x_recv,
    r_send,
    r_recv,
    h_send,
    h_recv,
    o_send,
    o_recv,
    f_send,
    f_recv,
    c_send,
    c_recv,
):
    dp = lax.axis_index("dp")
    tp = lax.axis_index("tensor")
    x, y = lax.rem(dp, NX), lax.div(dp, NX)
    c, z, h = lax.rem(tp, 2), lax.rem(lax.div(tp, 2), NZ), lax.div(tp, 2 * NZ)

    def dev_d(dx, dy):
        return {"dp": lax.rem(y + dy, NY) * NX + lax.rem(x + dx, NX), "tensor": tp}

    def t_of(hh, zz, cc):
        return (hh * NZ + zz) * 2 + cc

    def dev_t(dh, dz, dc=0):
        t = t_of(lax.rem(h + dh, NH), lax.rem(z + dz, NZ), lax.rem(c + dc, 2))
        return {"dp": dp, "tensor": t}

    x_next, x_prev, x_far = dev_d(1, 0), dev_d(NX - 1, 0), None
    y_other = dev_d(0, 1)
    sib = dev_t(0, 0, 1)
    h_other = dev_t(1, 0)
    z_next, z_prev = dev_t(0, 1), dev_t(0, NZ - 1)
    sent = []

    def send(src, dst, ssem, rsem, device):
        copy = pltpu.make_async_remote_copy(
            src_ref=src,
            dst_ref=dst,
            send_sem=ssem,
            recv_sem=rsem,
            device_id=device,
            device_id_type=MESH,
        )
        copy.start()
        sent.append(copy)

    def arrived(dst, ssem, rsem, device):
        pltpu.make_async_remote_copy(
            src_ref=dst,
            dst_ref=dst,
            send_sem=ssem,
            recv_sem=rsem,
            device_id=device,
            device_id_type=MESH,
        ).wait_recv()

    dp_others = [(dx, dy) for dx in (1, 3, 2, 0) for dy in (0, 1) if (dx, dy) != (0, 0)]
    tp_others = [(dh, dz) for dz in (2, 1, 3, 0) for dh in (1, 0) if (dh, dz) != (0, 0)]

    loads = [
        pltpu.make_async_copy(wg_ref, w.at[0], w_sem.at[0]),
        pltpu.make_async_copy(wu_ref, w.at[1], w_sem.at[1]),
        pltpu.make_async_copy(wd_ref, wd, w_sem.at[2]),
    ]
    for load in loads:
        load.start()
    mine = x * NY + y
    own = [
        pltpu.make_async_copy(
            x_ref.at[:, pl.ds(pl.multiple_of(dp * DS, DS), DS)], xb.at[tp, mine], l_sem.at[0]
        ),
        pltpu.make_async_copy(kb_ref, xb.at[tp, pl.ds(8, 2)], l_sem.at[1]),
    ]
    for copy in own:
        copy.start()

    barrier = pltpu.get_barrier_semaphore()
    for dx, dy in dp_others:
        pl.semaphore_signal(barrier, inc=1, device_id=dev_d(dx, dy), device_id_type=MESH)
    for dh, dz in tp_others:
        pl.semaphore_signal(barrier, inc=1, device_id=dev_t(dh, dz), device_id_type=MESH)
    pl.semaphore_signal(barrier, inc=1, device_id=sib, device_id_type=MESH)
    pl.semaphore_wait(barrier, len(dp_others) + len(tp_others) + 1)

    for i, (dx, dy) in enumerate(dp_others):
        there = lax.rem(y + dy, NY) * NX + lax.rem(x + dx, NX)
        send(
            x_ref.at[:, pl.ds(pl.multiple_of(there * DS, DS), DS)],
            xb.at[tp, mine],
            a_send.at[i],
            a_recv.at[mine],
            dev_d(dx, dy),
        )
    row = lax.broadcasted_iota(jnp.int32, (128, FU), 0)
    col = lax.broadcasted_iota(jnp.int32, (128, FU), 1)
    place = ((col & 31) >> 3) * 28 + (col >> 5)
    spread[...] = jnp.where(row == place, 1.0, 0.0).astype(BF16)
    for copy in own:
        copy.wait()
    for i, (dx, dy) in enumerate(dp_others):
        g = lax.rem(x + dx, NX) * NY + lax.rem(y + dy, NY)
        arrived(xb.at[tp, g], a_send.at[i], a_recv.at[g], dev_d(dx, dy))

    count = [0]

    def push(t, device):
        send(xb.at[t], xb.at[t], x_send.at[count[0]], x_recv.at[t], device)
        count[0] += 1

    def here(t):
        arrived(xb.at[t], x_send.at[0], x_recv.at[t], sib)

    z1, z3, z2 = lax.rem(z + 1, NZ), lax.rem(z + 3, NZ), lax.rem(z + 2, NZ)
    hh = 1 - h
    push(tp, h_other)
    push(tp, z_next)
    push(tp, z_prev)
    push(tp, sib)
    across = t_of(hh, z, c)
    here(across)
    push(across, z_next)
    push(across, z_prev)
    push(across, sib)

    def gather_near():
        a, b = t_of(h, z1, c), t_of(h, z3, c)
        e, f = t_of(hh, z1, c), t_of(hh, z3, c)
        here(a)
        push(a, z_prev)
        push(a, sib)
        here(b)
        push(b, sib)
        here(f)
        push(f, z_next)
        push(f, sib)
        here(e)
        push(e, sib)

    def gather_far():
        a, b = t_of(h, z2, c), t_of(hh, z2, c)
        here(a)
        push(a, sib)
        here(b)
        push(b, sib)

    xn1, xp1, xf = lax.rem(x + 1, NX), lax.rem(x + 3, NX), lax.rem(x + 2, NX)

    def matmul(k):
        zz = lax.rem(z + OFFSETS[k], NZ)
        here(t_of(0, zz, 1 - c))
        here(t_of(1, zz, 1 - c))
        blocks = [t_of(a, zz, b) for a in range(2) for b in range(2)]
        gain = gain_ref[...].astype(F32)
        for g in range(8):
            for i in range(4):
                v = xb[blocks[i], g].astype(F32) * gain
                xn[pl.ds(g * 32 + i * 8, 8), :] = v
        lhs = xn[...].astype(BF16)
        for half in range(2):
            if k == 0:
                loads[half].wait()
            acc = jnp.dot(lhs, w[half], preferred_element_type=F32).astype(BF16)
            for g in range(4):
                part[k, g, half] = acc[g * 64 : (g + 1) * 64]
            if half == 0:
                send(part.at[k, xf, 0], relay.at[k, 0], r_send.at[k, 0], r_recv.at[k, 0], x_next)
                send(part.at[k, xp1, 0], rx.at[k, 1, 0], r_send.at[k, 4], r_recv.at[k, 4], x_prev)
            else:
                send(part.at[k, xf, 1], relay.at[k, 1], r_send.at[k, 1], r_recv.at[k, 1], x_prev)
                send(part.at[k, xn1, 1], rx.at[k, 0, 1], r_send.at[k, 3], r_recv.at[k, 3], x_next)

    def relay_sums(k):
        arrived(relay.at[k, 0], r_send.at[k, 0], r_recv.at[k, 0], x_next)
        v = part[k, xn1, 0].astype(F32) + relay[k, 0].astype(F32)
        part[k, xn1, 0] = v.astype(BF16)
        send(part.at[k, xn1, 0], rx.at[k, 0, 0], r_send.at[k, 2], r_recv.at[k, 2], x_next)
        arrived(relay.at[k, 1], r_send.at[k, 1], r_recv.at[k, 1], x_prev)
        v = part[k, xp1, 1].astype(F32) + relay[k, 1].astype(F32)
        part[k, xp1, 1] = v.astype(BF16)
        send(part.at[k, xp1, 1], rx.at[k, 1, 1], r_send.at[k, 5], r_recv.at[k, 5], x_prev)

    def x_sum(k, half, rows):
        return (
            part[k, x, half, rows, :].astype(F32)
            + rx[k, 0, half, rows, :].astype(F32)
            + rx[k, 1, half, rows, :].astype(F32)
        )

    def y_sums(k):
        arrived(rx.at[k, 1, 0], r_send.at[k, 4], r_recv.at[k, 4], x_prev)
        arrived(rx.at[k, 0, 1], r_send.at[k, 3], r_recv.at[k, 3], x_next)
        arrived(rx.at[k, 0, 0], r_send.at[k, 2], r_recv.at[k, 2], x_next)
        arrived(rx.at[k, 1, 1], r_send.at[k, 5], r_recv.at[k, 5], x_prev)
        rows = pl.ds(pl.multiple_of((1 - y) * 32, 32), 32)
        for half in range(2):
            ysend[k, half] = x_sum(k, half, rows).astype(BF16)
        send(ysend.at[k], yrecv.at[k], r_send.at[k, 6], r_recv.at[k, 6], y_other)

    def hidden(k):
        zz = lax.rem(z + OFFSETS[k], NZ)
        lanes = pl.ds(pl.multiple_of(lax.rem(tp, 8) * 128, 128), 128)
        slots = jnp.concatenate(
            [
                xb[t_of(a, zz, b), 8 + lax.div(tp, 8), :, lanes].astype(F32)
                for a in range(2)
                for b in range(2)
            ],
            axis=0,
        )
        lane = lax.broadcasted_iota(jnp.int32, (32, 128), 1)
        inv = jnp.sum(
            jnp.where((lane >= 112) & (lane < 115), slots, 0.0), axis=1, keepdims=True
        )
        byte = jnp.dot(slots.astype(BF16), spread[...], preferred_element_type=F32)
        unit = lax.broadcasted_iota(jnp.int32, (32, FU), 1)
        bit = (byte.astype(jnp.int32) >> (unit & 7)) & 1
        keep = 2.0 * bit.astype(F32)
        arrived(yrecv.at[k], r_send.at[k, 6], r_recv.at[k, 6], y_other)
        rows = pl.ds(pl.multiple_of(y * 32, 32), 32)
        gate = (x_sum(k, 0, rows) + yrecv[k, 0].astype(F32)) * inv
        up = (x_sum(k, 1, rows) + yrecv[k, 1].astype(F32)) * inv
        hid[k, x, y] = (gate / (1.0 + jnp.exp(-gate)) * up * keep).astype(BF16)
        for i, device in enumerate((x_next, x_prev, y_other)):
            send(hid.at[k, x, y], hid.at[k, x, y], h_send.at[k, i], h_recv.at[k, mine], device)

    def h_here(k, xx, yy):
        arrived(hid.at[k, xx, yy], h_send.at[k, 0], h_recv.at[k, xx * NY + yy], x_next)

    def pass_y(k):
        h_here(k, x, 1 - y)
        for i, device in enumerate((x_next, x_prev)):
            send(
                hid.at[k, x, 1 - y],
                hid.at[k, x, 1 - y],
                h_send.at[k, 3 + i],
                h_recv.at[k, x * NY + 1 - y],
                device,
            )

    def pass_x(k):
        h_here(k, xp1, 0)
        send(
            hid.at[k, xp1, 0], hid.at[k, xp1, 0], h_send.at[k, 5], h_recv.at[k, xp1 * NY], x_next
        )
        h_here(k, xn1, 1)
        send(
            hid.at[k, xn1, 1],
            hid.at[k, xn1, 1],
            h_send.at[k, 6],
            h_recv.at[k, xn1 * NY + 1],
            x_prev,
        )

    def down(k):
        h_here(k, xp1, 1)
        h_here(k, xn1, 0)
        h_here(k, xf, 0)
        h_here(k, xf, 1)
        if k == 0:
            loads[2].wait()
        lhs = hid[k].reshape(256, FU)
        acc = jnp.dot(lhs, wd[...], preferred_element_type=F32).astype(BF16)
        for g in range(8):
            for s in range(2):
                osum[k, s, g] = acc[g * 32 + s * 16 : g * 32 + s * 16 + 16]
        send(osum.at[k, 1 - c], orecv.at[k], o_send.at[k], o_recv.at[k], sib)

    def to_owners(k):
        zz = lax.rem(z + OFFSETS[k], NZ)
        arrived(orecv.at[k], o_send.at[k], o_recv.at[k], sib)
        fsend[k] = (osum[k, c].astype(F32) + orecv[k].astype(F32)).astype(BF16)
        here_index = h * NZ + z
        for i, (dh, dz) in enumerate(tp_others):
            g = lax.rem(z + dz, NZ) * NY + lax.rem(h + dh, NH)
            send(
                fsend.at[k, g],
                frecv.at[here_index, zz],
                f_send.at[k, i],
                f_recv.at[here_index, zz],
                dev_t(dh, dz),
            )

    matmul(0)
    gather_near()
    matmul(1)
    relay_sums(0)
    matmul(2)
    gather_far()
    relay_sums(1)
    y_sums(0)
    matmul(3)
    relay_sums(2)
    y_sums(1)
    hidden(0)
    relay_sums(3)
    y_sums(2)
    hidden(1)
    pass_y(0)
    y_sums(3)
    hidden(2)
    pass_y(1)
    pass_x(0)
    hidden(3)
    pass_y(2)
    pass_x(1)
    down(0)
    pass_y(3)
    pass_x(2)
    down(1)
    to_owners(0)
    pass_x(3)
    down(2)
    to_owners(1)
    down(3)
    to_owners(2)
    to_owners(3)

    squares = []
    for k in range(4):
        zz = lax.rem(z + OFFSETS[k], NZ)
        total = fsend[k, z * NY + h].astype(F32)
        res = jnp.concatenate(
            [xb[t_of(c, zz, b), z * NY + h].astype(F32) for b in range(2)], axis=0
        )
        total = total + res
        for i, (dh, dz) in enumerate(tp_others):
            src = lax.rem(h + dh, NH) * NZ + lax.rem(z + dz, NZ)
            arrived(frecv.at[src, zz], f_send.at[0, i], f_recv.at[src, zz], dev_t(dh, dz))
            total = total + frecv[src, zz].astype(F32)
        rounded = total.astype(BF16)
        out_ref[pl.ds(pl.multiple_of(zz * 16, 16), 16), :] = rounded
    wide = out_ref[...].astype(F32)
    wide = wide * wide
    folded = wide[:, 0:128]
    for i in range(1, 8):
        folded = folded + wide[:, i * 128 : (i + 1) * 128]
    rowsum = jnp.sum(folded.T, axis=0, keepdims=True)
    csend[:, 0:64] = jnp.broadcast_to(rowsum, (8, 64))
    csend[:, 64:128] = jnp.zeros((8, 64), F32)
    for i, (dx, dy) in enumerate(dp_others):
        send(csend, crecv.at[mine], c_send.at[i], c_recv.at[mine], dev_d(dx, dy))
    total = csend[...]
    for i, (dx, dy) in enumerate(dp_others):
        g = lax.rem(x + dx, NX) * NY + lax.rem(y + dy, NY)
        arrived(crecv.at[g], c_send.at[i], c_recv.at[g], dev_d(dx, dy))
        total = total + crecv[g]
    rc_ref[...] = total / D
    for copy in sent:
        copy.wait_send()


def on_device(saved_input, keep_bits, norm_gain, gate_weight, up_weight, down_weight):
    rows = saved_input.shape[0]
    wide = saved_input.astype(F32)
    inv = lax.rsqrt(jnp.sum(wide * wide, axis=1) / D + 1e-05)
    hi = lax.reduce_precision(inv, 8, 7)
    mid = lax.reduce_precision(inv - hi, 8, 7)
    low = lax.reduce_precision(inv - hi - mid, 8, 7)
    words = keep_bits.reshape(rows, 16, 28)
    parts = [((words >> (8 * j)) & 255).astype(F32) for j in range(4)]
    scale = jnp.stack((hi, mid, low), axis=1)[:, None, :]
    parts.append(jnp.broadcast_to(scale, (rows, 16, 3)))
    parts.append(jnp.zeros((rows, 16, 13), F32))
    slots = jnp.concatenate(parts, axis=2).reshape(rows, 2, 1024).transpose(1, 0, 2)
    slots = slots.astype(BF16)
    vmem = pl.BlockSpec(memory_space=pltpu.VMEM)
    hbm = pl.BlockSpec(memory_space=pl.ANY)
    dma = pltpu.SemaphoreType.DMA
    out, check = pl.pallas_call(
        kernel,
        out_shape=(
            jax.ShapeDtypeStruct((64, DS), BF16),
            jax.ShapeDtypeStruct((8, 128), F32),
        ),
        in_specs=[vmem, vmem, vmem, hbm, hbm, hbm],
        out_specs=(vmem, vmem),
        scratch_shapes=[
            pltpu.VMEM((2, DS, FU), BF16),
            pltpu.VMEM((FU, DS), BF16),
            pltpu.VMEM((128, FU), BF16),
            pltpu.VMEM((16, 10, 8, DS), BF16),
            pltpu.VMEM((256, DS), F32),
            pltpu.VMEM((4, 4, 2, 64, FU), BF16),
            pltpu.VMEM((4, 2, 64, FU), BF16),
            pltpu.VMEM((4, 2, 2, 64, FU), BF16),
            pltpu.VMEM((4, 2, 32, FU), BF16),
            pltpu.VMEM((4, 2, 32, FU), BF16),
            pltpu.VMEM((4, 4, 2, 32, FU), BF16),
            pltpu.VMEM((4, 2, 8, 16, DS), BF16),
            pltpu.VMEM((4, 8, 16, DS), BF16),
            pltpu.VMEM((4, 8, 16, DS), BF16),
            pltpu.VMEM((8, 4, 16, DS), BF16),
            pltpu.VMEM((8, 128), F32),
            pltpu.VMEM((8, 8, 128), F32),
            dma((3,)),
            dma((2,)),
            dma((7,)),
            dma((8,)),
            dma((15,)),
            dma((16,)),
            dma((4, 7)),
            dma((4, 7)),
            dma((4, 7)),
            dma((4, 8)),
            dma((4,)),
            dma((4,)),
            dma((4, 7)),
            dma((8, 4)),
            dma((7,)),
            dma((8,)),
        ],
        compiler_params=pltpu.CompilerParams(
            collective_id=0, has_side_effects=True, vmem_limit_bytes=56 * 1024 * 1024
        ),
        name="block",
    )(saved_input, slots, norm_gain.reshape(1, DS), gate_weight, up_weight, down_weight)
    return out, check[0, :64]


def solution(mesh):
    both = ("dp", "tensor")
    return jax.shard_map(
        on_device,
        mesh=mesh,
        in_specs=(
            P(both, None),
            P(both, None),
            P("dp"),
            P("dp", "tensor"),
            P("dp", "tensor"),
            P("tensor", "dp"),
        ),
        out_specs=(P("tensor", "dp"), P("tensor")),
        check_vma=False,
    )
```

time: 201 us -> 94.3 us (0.47); the launches traced: 198 us -> 94.1 us
  Pallas kernels: 0 us -> 86.3 us
  blocking collectives: 83.2 us -> 0 us
  waiting for transfers between devices: 51.5 us -> 0 us
  starting transfers between devices: 14.5 us -> 0 us
  between operations: 14.3 us -> 0.69 us
  local copies, waits for them, and re-layouts: 16 us -> 5.29 us
  matrix products: 9.25 us -> 0 us
  other arithmetic: 9.45 us -> 1.84 us
    pallas_call x0 -> x1, Pallas kernels: none -> 86.3 us  [on_device(): pl.pallas_call(kernel, out_shape=(jax.ShapeDtypeStruct((64, DS), BF16), j...]
    all_to_all x6 -> x0, blocking collectives: 83.2 us -> none  [the longest x4 62.3 us: sent_to_all(): lax.all_to_all(jnp.broadcast_to(value[None], (length, *value.shape)), axi...]
    unnamed x2 -> x0, waiting for transfers between devices: 27.7 us -> none
    all_to_all x3 -> x0, waiting for transfers between devices: 23.8 us -> none  [the longest x1 14.5 us: sum_in_two_steps(): lax.all_to_all(nearer.astype(jnp.bfloat16), far, split_axis=0, concat_axi...]
    all_to_all x3 -> x0, starting transfers between devices: 14.4 us -> none  [the longest x1 6.26 us: sum_in_two_steps(): lax.all_to_all(nearer.astype(jnp.bfloat16), far, split_axis=0, concat_axi...]
    dot_general x3 -> x0, matrix products: 9.25 us -> none  [the longest x1 4.58 us: on_device(): up_part = jnp.dot(normed, up_weight, preferred_element_type=jnp.float32)]
    unnamed x16 -> x1, local copies, waits for them, and re-layouts: 10.1 us -> 1.57 us
    reduce_sum x6 -> x1, other arithmetic: 5.76 us -> 1.09 us  [on_device(): inv = lax.rsqrt(jnp.sum(wide * wide, axis=1) / D + 1e-05)]
  transfers between devices with their start and end apart: 4 -> 0, of which waited for: 4 -> 0; matrix products, arithmetic and copies ran while one was open for 3% -> 0% of each run, Pallas kernels for 0% -> 0%
where the time goes in v1:
time: 94.3 us; the launch traced here: 94.1 us
  Pallas kernels  86.3 us (92%)
  local copies, waits for them, and re-layouts  5.29 us (6%)
  other arithmetic  1.84 us (2%)
    pallas_call x1, Pallas kernels, on_device(): pl.pallas_call(kernel, out_shape=(jax.ShapeDtypeStruct((64, DS), BF16), j...  86.3 us

profile of v1, /device:TPU:1, one launch (start us, length us, event | category | flops | bytes accessed | tf_op | source)
XLA Modules:
  0.0 94.1 jit_solution(17524113461992892686)
XLA Ops:
  0.6 1.1 %multiply_reduce_fusion = f32[8]{0:T(128)S(1)} fusion(bf16[8,8192]{1,0:T(8,128)(2,1)} %x_ref.1), kind=kLoop, calls=%fused_computation | loop fusion | flops 196600 | bytes 131104 | tf_op jit(solution)/shard_map/reduce_sum | solution.py:403
  1.7 0.1 copy.9
  1.8 1.3 %reshape.76.gain_ref = bf16[1,1024]{1,0:T(2,128)(2,1)} reshape(bf16[1024]{0:T(1024)(128)(2,1)} %param.8) | data formatting | bytes 4096 | tf_op jit(solution)/shard_map/reshape | solution.py:464
  3.1 0.7 convert_convert_fusion
  3.9 0.1 convert_element_type.39
  4.0 0.1 convert_element_type.35
  4.1 0.1 convert_element_type.33
  4.2 0.1 convert_element_type.37
  4.3 0.1 concatenate.4
  4.4 0.6 copy.12
  5.1 86.3 %block.1 = (bf16[64,1024]{1,0:T(8,128)(2,1)}, f32[8,128]{1,0:T(8,128)}) custom-call(bf16[8,8192]{1,0:T(8,128)(2,1)} %x_ref.1, bf16[2,8,1024]{2,1,0:T(8,128)(2,1)} %bitcast.18, bf16[1,1024]{1,0:T(2,128)(2,1)} %reshape.76.gain_ref, bf16[1024,896]{1,0:T(8,128)(2,1)} %wg_ref.1, bf16[1024,896]{1,0:T(8,128)(2,1)} %wu_ref.1, bf16[896,1024]{1,0:T(8,128)(2,1)} %wd_ref.1), custom_call_target="tpu_custom_call" | custom-call | tf_op jit(solution)/shard_map/block/pallas_call | solution.py:417
  91.3 1.2 %slice_bitcast_fusion = f32[64]{0:T(128)} fusion(f32[8,128]{1,0:T(8,128)} %get-tuple-element.5), kind=kLoop, calls=%fused_computation.9 | loop fusion | bytes 512 | tf_op jit(solution)/shard_map/squeeze | solution.py:465
  92.5 1.6 %copy.14 = bf16[64,1024]{1,0:T(8,128)(2,1)} copy(bf16[64,1024]{1,0:T(8,128)(2,1)} %get-tuple-element.15) | data formatting | bytes 262144
  (5 shorter events, 0.1 us)

commit v2 on v1

--- a/solution.py
+++ b/solution.py
@@ -19,19 +19,25 @@
     x_ref,
     kb_ref,
     gain_ref,
-    wg_ref,
-    wu_ref,
-    wd_ref,
+    wg_hbm,
+    wu_hbm,
+    wd_hbm,
     out_ref,
     rc_ref,
-    w,
+    wg,
+    wu,
     wd,
     spread,
+    words,
     xb,
     xn,
-    part,
-    relay,
-    rx,
+    pg,
+    pu,
+    g_relay,
+    g_recv,
+    u_relay,
+    u_recv,
+    u_y,
     ysend,
     yrecv,
     hid,
@@ -47,8 +53,10 @@
     a_recv,
     x_send,
     x_recv,
-    r_send,
-    r_recv,
+    g_send,
+    g_done,
+    u_send,
+    u_done,
     h_send,
     h_recv,
     o_send,
@@ -73,7 +81,7 @@
         t = t_of(lax.rem(h + dh, NH), lax.rem(z + dz, NZ), lax.rem(c + dc, 2))
         return {"dp": dp, "tensor": t}
 
-    x_next, x_prev, x_far = dev_d(1, 0), dev_d(NX - 1, 0), None
+    x_next, x_prev = dev_d(1, 0), dev_d(NX - 1, 0)
     y_other = dev_d(0, 1)
     sib = dev_t(0, 0, 1)
     h_other = dev_t(1, 0)
@@ -106,21 +114,17 @@
     tp_others = [(dh, dz) for dz in (2, 1, 3, 0) for dh in (1, 0) if (dh, dz) != (0, 0)]
 
     loads = [
-        pltpu.make_async_copy(wg_ref, w.at[0], w_sem.at[0]),
-        pltpu.make_async_copy(wu_ref, w.at[1], w_sem.at[1]),
-        pltpu.make_async_copy(wd_ref, wd, w_sem.at[2]),
+        pltpu.make_async_copy(wu_hbm, wu, w_sem.at[0]),
+        pltpu.make_async_copy(wg_hbm, wg, w_sem.at[1]),
+        pltpu.make_async_copy(wd_hbm, wd, w_sem.at[2]),
     ]
     for load in loads:
         load.start()
     mine = x * NY + y
-    own = [
-        pltpu.make_async_copy(
-            x_ref.at[:, pl.ds(pl.multiple_of(dp * DS, DS), DS)], xb.at[tp, mine], l_sem.at[0]
-        ),
-        pltpu.make_async_copy(kb_ref, xb.at[tp, pl.ds(8, 2)], l_sem.at[1]),
-    ]
-    for copy in own:
-        copy.start()
+    own = pltpu.make_async_copy(
+        x_ref.at[:, pl.ds(pl.multiple_of(dp * DS, DS), DS)], xb.at[tp, mine], l_sem
+    )
+    own.start()
 
     barrier = pltpu.get_barrier_semaphore()
     for dx, dy in dp_others:
@@ -128,6 +132,32 @@
     for dh, dz in tp_others:
         pl.semaphore_signal(barrier, inc=1, device_id=dev_t(dh, dz), device_id_type=MESH)
     pl.semaphore_signal(barrier, inc=1, device_id=sib, device_id_type=MESH)
+    wide = x_ref[...].astype(F32)
+    inv = lax.rsqrt(jnp.sum(wide * wide, axis=1, keepdims=True) / D + 1e-05)
+    hi = inv.astype(BF16).astype(F32)
+    mid = (inv - hi).astype(BF16).astype(F32)
+    low = inv - hi - mid
+    words[...] = jnp.zeros((8, 512), jnp.int32)
+    words[:, 0:448] = kb_ref[...]
+    lane = lax.broadcasted_iota(jnp.int32, (8, 128), 1)
+    scale = jnp.where(lane == 112, hi, jnp.where(lane == 113, mid, low))
+    scale = jnp.where((lane >= 112) & (lane < 115), scale, 0.0)
+    for t in range(16):
+        tile, start = divmod(28 * t, 128)
+        piece = words[:, tile * 128 : tile * 128 + 128]
+        if start:
+            piece = pltpu.roll(piece, 128 - start, 1)
+        if start + 28 > 128:
+            after = pltpu.roll(words[:, tile * 128 + 128 : tile * 128 + 256], 128 - start, 1)
+            piece = jnp.where(lane < 128 - start, piece, after)
+        taken = jnp.zeros((8, 128), jnp.int32)
+        for j in range(4):
+            byte = (piece >> (8 * j)) & 255
+            if j:
+                byte = pltpu.roll(byte, 28 * j, 1)
+            taken = jnp.where((lane >= 28 * j) & (lane < 28 * j + 28), byte, taken)
+        slot = (taken.astype(F32) + scale).astype(BF16)
+        xb[tp, 8 + t // 8, :, (t % 8) * 128 : (t % 8) * 128 + 128] = slot
     pl.semaphore_wait(barrier, len(dp_others) + len(tp_others) + 1)
 
     for i, (dx, dy) in enumerate(dp_others):
@@ -143,8 +173,7 @@
     col = lax.broadcasted_iota(jnp.int32, (128, FU), 1)
     place = ((col & 31) >> 3) * 28 + (col >> 5)
     spread[...] = jnp.where(row == place, 1.0, 0.0).astype(BF16)
-    for copy in own:
-        copy.wait()
+    own.wait()
     for i, (dx, dy) in enumerate(dp_others):
         g = lax.rem(x + dx, NX) * NY + lax.rem(y + dy, NY)
         arrived(xb.at[tp, g], a_send.at[i], a_recv.at[g], dev_d(dx, dy))
@@ -198,51 +227,79 @@
         here(t_of(0, zz, 1 - c))
         here(t_of(1, zz, 1 - c))
         blocks = [t_of(a, zz, b) for a in range(2) for b in range(2)]
-        gain = gain_ref[...].astype(F32)
+        gain = gain_ref[...].astype(F32).reshape(1, DS)
         for g in range(8):
             for i in range(4):
                 v = xb[blocks[i], g].astype(F32) * gain
                 xn[pl.ds(g * 32 + i * 8, 8), :] = v
         lhs = xn[...].astype(BF16)
-        for half in range(2):
-            if k == 0:
-                loads[half].wait()
-            acc = jnp.dot(lhs, w[half], preferred_element_type=F32).astype(BF16)
-            for g in range(4):
-                part[k, g, half] = acc[g * 64 : (g + 1) * 64]
-            if half == 0:
-                send(part.at[k, xf, 0], relay.at[k, 0], r_send.at[k, 0], r_recv.at[k, 0], x_next)
-                send(part.at[k, xp1, 0], rx.at[k, 1, 0], r_send.at[k, 4], r_recv.at[k, 4], x_prev)
-            else:
-                send(part.at[k, xf, 1], relay.at[k, 1], r_send.at[k, 1], r_recv.at[k, 1], x_prev)
-                send(part.at[k, xn1, 1], rx.at[k, 0, 1], r_send.at[k, 3], r_recv.at[k, 3], x_next)
-
-    def relay_sums(k):
-        arrived(relay.at[k, 0], r_send.at[k, 0], r_recv.at[k, 0], x_next)
-        v = part[k, xn1, 0].astype(F32) + relay[k, 0].astype(F32)
-        part[k, xn1, 0] = v.astype(BF16)
-        send(part.at[k, xn1, 0], rx.at[k, 0, 0], r_send.at[k, 2], r_recv.at[k, 2], x_next)
-        arrived(relay.at[k, 1], r_send.at[k, 1], r_recv.at[k, 1], x_prev)
-        v = part[k, xp1, 1].astype(F32) + relay[k, 1].astype(F32)
-        part[k, xp1, 1] = v.astype(BF16)
-        send(part.at[k, xp1, 1], rx.at[k, 1, 1], r_send.at[k, 5], r_recv.at[k, 5], x_prev)
-
-    def x_sum(k, half, rows):
+        if k == 0:
+            loads[0].wait()
+        acc = jnp.dot(lhs, wu[...], preferred_element_type=F32).astype(BF16)
+        for g in range(8):
+            for i in range(2):
+                lo = g * 32 + i * 16
+                pu[k, g % 2, g // 2, i] = acc[lo : lo + 16]
+        send(pu.at[k, 1 - y], u_y.at[k], u_send.at[k, 0], u_done.at[k, 0], y_other)
+        if k == 0:
+            loads[1].wait()
+        acc = jnp.dot(lhs, wg[...], preferred_element_type=F32).astype(BF16)
+        for g in range(8):
+            pg[k, g // 2, g % 2] = acc[g * 32 : g * 32 + 32]
+        send(pg.at[k, xf, 0], g_relay.at[k, 0], g_send.at[k, 0], g_done.at[k, 0], x_next)
+        send(pg.at[k, xf, 1], g_relay.at[k, 1], g_send.at[k, 1], g_done.at[k, 1], x_prev)
+        send(pg.at[k, xn1, 1], g_recv.at[k, 0, 1], g_send.at[k, 3], g_done.at[k, 3], x_next)
+        send(pg.at[k, xp1, 0], g_recv.at[k, 1, 0], g_send.at[k, 4], g_done.at[k, 4], x_prev)
+
+    def gate_relay(k):
+        arrived(g_relay.at[k, 0], g_send.at[k, 0], g_done.at[k, 0], x_next)
+        v = pg[k, xn1, 0].astype(F32) + g_relay[k, 0].astype(F32)
+        pg[k, xn1, 0] = v.astype(BF16)
+        send(pg.at[k, xn1, 0], g_recv.at[k, 0, 0], g_send.at[k, 2], g_done.at[k, 2], x_next)
+        arrived(g_relay.at[k, 1], g_send.at[k, 1], g_done.at[k, 1], x_prev)
+        v = pg[k, xp1, 1].astype(F32) + g_relay[k, 1].astype(F32)
+        pg[k, xp1, 1] = v.astype(BF16)
+        send(pg.at[k, xp1, 1], g_recv.at[k, 1, 1], g_send.at[k, 5], g_done.at[k, 5], x_prev)
+
+    def gate_over_x(k, yy):
         return (
-            part[k, x, half, rows, :].astype(F32)
-            + rx[k, 0, half, rows, :].astype(F32)
-            + rx[k, 1, half, rows, :].astype(F32)
-        )
-
-    def y_sums(k):
-        arrived(rx.at[k, 1, 0], r_send.at[k, 4], r_recv.at[k, 4], x_prev)
-        arrived(rx.at[k, 0, 1], r_send.at[k, 3], r_recv.at[k, 3], x_next)
-        arrived(rx.at[k, 0, 0], r_send.at[k, 2], r_recv.at[k, 2], x_next)
-        arrived(rx.at[k, 1, 1], r_send.at[k, 5], r_recv.at[k, 5], x_prev)
-        rows = pl.ds(pl.multiple_of((1 - y) * 32, 32), 32)
-        for half in range(2):
-            ysend[k, half] = x_sum(k, half, rows).astype(BF16)
-        send(ysend.at[k], yrecv.at[k], r_send.at[k, 6], r_recv.at[k, 6], y_other)
+            pg[k, x, yy].astype(F32) + g_recv[k, 0, yy].astype(F32) + g_recv[k, 1, yy].astype(F32)
+        )
+
+    def gate_y(k):
+        arrived(g_recv.at[k, 0, 1], g_send.at[k, 3], g_done.at[k, 3], x_next)
+        arrived(g_recv.at[k, 1, 0], g_send.at[k, 4], g_done.at[k, 4], x_prev)
+        arrived(g_recv.at[k, 0, 0], g_send.at[k, 2], g_done.at[k, 2], x_next)
+        arrived(g_recv.at[k, 1, 1], g_send.at[k, 5], g_done.at[k, 5], x_prev)
+        ysend[k] = gate_over_x(k, 1 - y).astype(BF16)
+        send(ysend.at[k], yrecv.at[k], g_send.at[k, 6], g_done.at[k, 6], y_other)
+
+    def up_over_y(k):
+        arrived(u_y.at[k], u_send.at[k, 0], u_done.at[k, 0], y_other)
+        for xx in (xf, xn1, xp1, x):
+            v = pu[k, y, xx].astype(F32) + u_y[k, xx].astype(F32)
+            pu[k, y, xx] = v.astype(BF16)
+            if xx is xf:
+                send(pu.at[k, y, xf, 0], u_relay.at[k, 0], u_send.at[k, 1], u_done.at[k, 1], x_next)
+                send(pu.at[k, y, xf, 1], u_relay.at[k, 1], u_send.at[k, 2], u_done.at[k, 2], x_prev)
+            if xx is xn1:
+                send(
+                    pu.at[k, y, xx, 1], u_recv.at[k, 0, 1], u_send.at[k, 3], u_done.at[k, 3], x_next
+                )
+            if xx is xp1:
+                send(
+                    pu.at[k, y, xx, 0], u_recv.at[k, 1, 0], u_send.at[k, 4], u_done.at[k, 4], x_prev
+                )
+
+    def up_relay(k):
+        arrived(u_relay.at[k, 0], u_send.at[k, 1], u_done.at[k, 1], x_next)
+        v = pu[k, y, xn1, 0].astype(F32) + u_relay[k, 0].astype(F32)
+        pu[k, y, xn1, 0] = v.astype(BF16)
+        send(pu.at[k, y, xn1, 0], u_recv.at[k, 0, 0], u_send.at[k, 5], u_done.at[k, 5], x_next)
+        arrived(u_relay.at[k, 1], u_send.at[k, 2], u_done.at[k, 2], x_prev)
+        v = pu[k, y, xp1, 1].astype(F32) + u_relay[k, 1].astype(F32)
+        pu[k, y, xp1, 1] = v.astype(BF16)
+        send(pu.at[k, y, xp1, 1], u_recv.at[k, 1, 1], u_send.at[k, 6], u_done.at[k, 6], x_prev)
 
     def hidden(k):
         zz = lax.rem(z + OFFSETS[k], NZ)
@@ -263,10 +320,14 @@
         unit = lax.broadcasted_iota(jnp.int32, (32, FU), 1)
         bit = (byte.astype(jnp.int32) >> (unit & 7)) & 1
         keep = 2.0 * bit.astype(F32)
-        arrived(yrecv.at[k], r_send.at[k, 6], r_recv.at[k, 6], y_other)
-        rows = pl.ds(pl.multiple_of(y * 32, 32), 32)
-        gate = (x_sum(k, 0, rows) + yrecv[k, 0].astype(F32)) * inv
-        up = (x_sum(k, 1, rows) + yrecv[k, 1].astype(F32)) * inv
+        arrived(yrecv.at[k], g_send.at[k, 6], g_done.at[k, 6], y_other)
+        gate = (gate_over_x(k, y) + yrecv[k].astype(F32)) * inv
+        arrived(u_recv.at[k, 0, 1], u_send.at[k, 3], u_done.at[k, 3], x_next)
+        arrived(u_recv.at[k, 1, 0], u_send.at[k, 4], u_done.at[k, 4], x_prev)
+        arrived(u_recv.at[k, 0, 0], u_send.at[k, 5], u_done.at[k, 5], x_next)
+        arrived(u_recv.at[k, 1, 1], u_send.at[k, 6], u_done.at[k, 6], x_prev)
+        up = pu[k, y, x].astype(F32) + u_recv[k, 0].astype(F32) + u_recv[k, 1].astype(F32)
+        up = up.reshape(32, FU) * inv
         hid[k, x, y] = (gate / (1.0 + jnp.exp(-gate)) * up * keep).astype(BF16)
         for i, device in enumerate((x_next, x_prev, y_other)):
             send(hid.at[k, x, y], hid.at[k, x, y], h_send.at[k, i], h_recv.at[k, mine], device)
@@ -330,40 +391,47 @@
 
     matmul(0)
     gather_near()
+    gate_relay(0)
+    matmul(2)
     matmul(1)
-    relay_sums(0)
-    matmul(2)
+    gate_y(0)
+    up_over_y(0)
     gather_far()
-    relay_sums(1)
-    y_sums(0)
     matmul(3)
-    relay_sums(2)
-    y_sums(1)
+    up_over_y(2)
+    gate_relay(3)
+    up_relay(0)
+    up_over_y(1)
+    gate_relay(1)
+    gate_relay(2)
     hidden(0)
-    relay_sums(3)
-    y_sums(2)
+    up_relay(1)
+    up_relay(2)
+    gate_y(1)
+    gate_y(2)
+    up_over_y(3)
+    gate_y(3)
+    pass_y(0)
     hidden(1)
-    pass_y(0)
-    y_sums(3)
     hidden(2)
+    pass_x(0)
     pass_y(1)
-    pass_x(0)
+    up_relay(3)
+    pass_y(2)
+    down(0)
+    pass_x(1)
     hidden(3)
-    pass_y(2)
-    pass_x(1)
-    down(0)
+    pass_x(2)
+    to_owners(0)
+    down(1)
     pass_y(3)
-    pass_x(2)
-    down(1)
-    to_owners(0)
+    to_owners(1)
+    down(2)
     pass_x(3)
-    down(2)
-    to_owners(1)
+    to_owners(2)
     down(3)
-    to_owners(2)
     to_owners(3)
 
-    squares = []
     for k in range(4):
         zz = lax.rem(z + OFFSETS[k], NZ)
         total = fsend[k, z * NY + h].astype(F32)
@@ -392,25 +460,12 @@
         g = lax.rem(x + dx, NX) * NY + lax.rem(y + dy, NY)
         arrived(crecv.at[g], c_send.at[i], c_recv.at[g], dev_d(dx, dy))
         total = total + crecv[g]
-    rc_ref[...] = total / D
+    rc_ref[...] = total[0, 0:64] / D
     for copy in sent:
         copy.wait_send()
 
 
 def on_device(saved_input, keep_bits, norm_gain, gate_weight, up_weight, down_weight):
-    rows = saved_input.shape[0]
-    wide = saved_input.astype(F32)
-    inv = lax.rsqrt(jnp.sum(wide * wide, axis=1) / D + 1e-05)
-    hi = lax.reduce_precision(inv, 8, 7)
-    mid = lax.reduce_precision(inv - hi, 8, 7)
-    low = lax.reduce_precision(inv - hi - mid, 8, 7)
-    words = keep_bits.reshape(rows, 16, 28)
-    parts = [((words >> (8 * j)) & 255).astype(F32) for j in range(4)]
-    scale = jnp.stack((hi, mid, low), axis=1)[:, None, :]
-    parts.append(jnp.broadcast_to(scale, (rows, 16, 3)))
-    parts.append(jnp.zeros((rows, 16, 13), F32))
-    slots = jnp.concatenate(parts, axis=2).reshape(rows, 2, 1024).transpose(1, 0, 2)
-    slots = slots.astype(BF16)
     vmem = pl.BlockSpec(memory_space=pltpu.VMEM)
     hbm = pl.BlockSpec(memory_space=pl.ANY)
     dma = pltpu.SemaphoreType.DMA
@@ -418,21 +473,27 @@
         kernel,
         out_shape=(
             jax.ShapeDtypeStruct((64, DS), BF16),
-            jax.ShapeDtypeStruct((8, 128), F32),
+            jax.ShapeDtypeStruct((64,), F32),
         ),
         in_specs=[vmem, vmem, vmem, hbm, hbm, hbm],
         out_specs=(vmem, vmem),
         scratch_shapes=[
-            pltpu.VMEM((2, DS, FU), BF16),
+            pltpu.VMEM((DS, FU), BF16),
+            pltpu.VMEM((DS, FU), BF16),
             pltpu.VMEM((FU, DS), BF16),
             pltpu.VMEM((128, FU), BF16),
+            pltpu.VMEM((8, 512), jnp.int32),
             pltpu.VMEM((16, 10, 8, DS), BF16),
             pltpu.VMEM((256, DS), F32),
-            pltpu.VMEM((4, 4, 2, 64, FU), BF16),
-            pltpu.VMEM((4, 2, 64, FU), BF16),
-            pltpu.VMEM((4, 2, 2, 64, FU), BF16),
+            pltpu.VMEM((4, 4, 2, 32, FU), BF16),
+            pltpu.VMEM((4, 2, 4, 2, 16, FU), BF16),
             pltpu.VMEM((4, 2, 32, FU), BF16),
-            pltpu.VMEM((4, 2, 32, FU), BF16),
+            pltpu.VMEM((4, 2, 2, 32, FU), BF16),
+            pltpu.VMEM((4, 2, 16, FU), BF16),
+            pltpu.VMEM((4, 2, 2, 16, FU), BF16),
+            pltpu.VMEM((4, 4, 2, 16, FU), BF16),
+            pltpu.VMEM((4, 32, FU), BF16),
+            pltpu.VMEM((4, 32, FU), BF16),
             pltpu.VMEM((4, 4, 2, 32, FU), BF16),
             pltpu.VMEM((4, 2, 8, 16, DS), BF16),
             pltpu.VMEM((4, 8, 16, DS), BF16),
@@ -441,11 +502,13 @@
             pltpu.VMEM((8, 128), F32),
             pltpu.VMEM((8, 8, 128), F32),
             dma((3,)),
-            dma((2,)),
+            dma,
             dma((7,)),
             dma((8,)),
             dma((15,)),
             dma((16,)),
+            dma((4, 7)),
+            dma((4, 7)),
             dma((4, 7)),
             dma((4, 7)),
             dma((4, 7)),
@@ -461,8 +524,8 @@
             collective_id=0, has_side_effects=True, vmem_limit_bytes=56 * 1024 * 1024
         ),
         name="block",
-    )(saved_input, slots, norm_gain.reshape(1, DS), gate_weight, up_weight, down_weight)
-    return out, check[0, :64]
+    )(saved_input, keep_bits, norm_gain, gate_weight, up_weight, down_weight)
+    return out, check
 
 
 def solution(mesh):

time: 94.3 us -> 84.7 us (0.90)
  Pallas kernels: 86.3 us -> 81.2 us
  local copies, waits for them, and re-layouts: 5.29 us -> 2.74 us
  other arithmetic: 1.84 us -> 0 us
    pallas_call x1, Pallas kernels: 86.3 us -> 81.2 us  [on_device(): pl.pallas_call(kernel, out_shape=(jax.ShapeDtypeStruct((64, DS), BF16), j...]
    reshape x1 -> x0, local copies, waits for them, and re-layouts: 1.28 us -> none  [on_device(): norm_gain.reshape(1, DS)]
    squeeze x1 -> x0, local copies, waits for them, and re-layouts: 1.18 us -> none  [on_device(): return (out, check[0, :64])]
    unnamed x1 -> x2, local copies, waits for them, and re-layouts: 1.57 us -> 2.74 us
    reduce_sum x1 -> x0, other arithmetic: 1.09 us -> none  [on_device(): inv = lax.rsqrt(jnp.sum(wide * wide, axis=1) / D + 1e-05)]
    convert_element_type x6 -> x0, local copies, waits for them, and re-layouts: 1.01 us -> none  [the longest x2 0.64 us: on_device(): slots = slots.astype(BF16)]
where the time goes in v2:
time: 84.7 us; the launch traced here: 84.6 us
  Pallas kernels  81.2 us (96%)
  local copies, waits for them, and re-layouts  2.74 us (3%)
    pallas_call x1, Pallas kernels, on_device(): pl.pallas_call(kernel, out_shape=(jax.ShapeDtypeStruct((64, DS), BF16), j...  81.2 us
    unnamed x2, local copies, waits for them, and re-layouts  2.74 us

profile of v2, /device:TPU:1, one launch (start us, length us, event | category | flops | bytes accessed | tf_op | source)
XLA Modules:
  0.0 84.6 jit_solution(16164107927982045127)
XLA Ops:
  0.6 81.2 %block.1 = (bf16[64,1024]{1,0:T(8,128)(2,1)}, f32[64]{0:T(128)}) custom-call(bf16[8,8192]{1,0:T(8,128)(2,1)} %x_ref.1, s32[8,448]{1,0:T(8,128)} %kb_ref.1, bf16[1024]{0:T(1024)(128)(2,1)} %gain_ref.1, bf16[1024,896]{1,0:T(8,128)(2,1)} %wg_hbm.1, bf16[1024,896]{1,0:T(8,128)(2,1)} %wu_hbm.1, bf16[896,1024]{1,0:T(8,128)(2,1)} %wd_hbm.1), custom_call_target="tpu_custom_call" | custom-call | tf_op jit(solution)/shard_map/block/pallas_call | solution.py:472
  81.8 1.6 %copy.10 = bf16[64,1024]{1,0:T(8,128)(2,1)} copy(bf16[64,1024]{1,0:T(8,128)(2,1)} %get-tuple-element.4) | data formatting | bytes 262144
  83.4 1.2 %copy.11 = f32[64]{0:T(128)} copy(f32[64]{0:T(128)} %get-tuple-element.5) | data formatting | bytes 512

commit v3 on v2

--- a/solution.py
+++ b/solution.py
@@ -16,7 +16,7 @@
 
 
 def kernel(
-    x_ref,
+    x_hbm,
     kb_ref,
     gain_ref,
     wg_hbm,
@@ -29,6 +29,7 @@
     wd,
     spread,
     words,
+    x_ref,
     xb,
     xn,
     pg,
@@ -51,6 +52,7 @@
     l_sem,
     a_send,
     a_recv,
+    k_sem,
     x_send,
     x_recv,
     g_send,
@@ -71,11 +73,12 @@
     x, y = lax.rem(dp, NX), lax.div(dp, NX)
     c, z, h = lax.rem(tp, 2), lax.rem(lax.div(tp, 2), NZ), lax.div(tp, 2 * NZ)
 
-    def dev_d(dx, dy):
-        return {"dp": lax.rem(y + dy, NY) * NX + lax.rem(x + dx, NX), "tensor": tp}
-
     def t_of(hh, zz, cc):
         return (hh * NZ + zz) * 2 + cc
+
+    def dev_d(dx, dy, dh=0):
+        d = lax.rem(y + dy, NY) * NX + lax.rem(x + dx, NX)
+        return {"dp": d, "tensor": t_of(lax.rem(h + dh, NH), z, c)}
 
     def dev_t(dh, dz, dc=0):
         t = t_of(lax.rem(h + dh, NH), lax.rem(z + dz, NZ), lax.rem(c + dc, 2))
@@ -113,25 +116,31 @@
     dp_others = [(dx, dy) for dx in (1, 3, 2, 0) for dy in (0, 1) if (dx, dy) != (0, 0)]
     tp_others = [(dh, dz) for dz in (2, 1, 3, 0) for dh in (1, 0) if (dh, dz) != (0, 0)]
 
+    row_others = [(dx, dy, 0) for dx, dy in dp_others]
+    row_others += [(dx, dy, 1) for dx, dy in [*dp_others, (0, 0)]]
+
     loads = [
         pltpu.make_async_copy(wu_hbm, wu, w_sem.at[0]),
         pltpu.make_async_copy(wg_hbm, wg, w_sem.at[1]),
         pltpu.make_async_copy(wd_hbm, wd, w_sem.at[2]),
     ]
-    for load in loads:
-        load.start()
+    rows_in = pltpu.make_async_copy(x_hbm, x_ref, l_sem.at[0])
+    rows_in.start()
     mine = x * NY + y
+
+    barrier = pltpu.get_barrier_semaphore()
+    for dx, dy, dh in row_others:
+        pl.semaphore_signal(barrier, inc=1, device_id=dev_d(dx, dy, dh), device_id_type=MESH)
+    for dh, dz in tp_others:
+        if dz == 0:
+            continue
+        pl.semaphore_signal(barrier, inc=1, device_id=dev_t(dh, dz), device_id_type=MESH)
+    pl.semaphore_signal(barrier, inc=1, device_id=sib, device_id_type=MESH)
+    rows_in.wait()
     own = pltpu.make_async_copy(
-        x_ref.at[:, pl.ds(pl.multiple_of(dp * DS, DS), DS)], xb.at[tp, mine], l_sem
+        x_ref.at[:, pl.ds(pl.multiple_of(dp * DS, DS), DS)], xb.at[tp, mine], l_sem.at[1]
     )
     own.start()
-
-    barrier = pltpu.get_barrier_semaphore()
-    for dx, dy in dp_others:
-        pl.semaphore_signal(barrier, inc=1, device_id=dev_d(dx, dy), device_id_type=MESH)
-    for dh, dz in tp_others:
-        pl.semaphore_signal(barrier, inc=1, device_id=dev_t(dh, dz), device_id_type=MESH)
-    pl.semaphore_signal(barrier, inc=1, device_id=sib, device_id_type=MESH)
     wide = x_ref[...].astype(F32)
     inv = lax.rsqrt(jnp.sum(wide * wide, axis=1, keepdims=True) / D + 1e-05)
     hi = inv.astype(BF16).astype(F32)
@@ -158,26 +167,24 @@
             taken = jnp.where((lane >= 28 * j) & (lane < 28 * j + 28), byte, taken)
         slot = (taken.astype(F32) + scale).astype(BF16)
         xb[tp, 8 + t // 8, :, (t % 8) * 128 : (t % 8) * 128 + 128] = slot
-    pl.semaphore_wait(barrier, len(dp_others) + len(tp_others) + 1)
-
-    for i, (dx, dy) in enumerate(dp_others):
+    pl.semaphore_wait(barrier, len(row_others) + 7)
+
+    for i, (dx, dy, dh) in enumerate(row_others):
         there = lax.rem(y + dy, NY) * NX + lax.rem(x + dx, NX)
         send(
             x_ref.at[:, pl.ds(pl.multiple_of(there * DS, DS), DS)],
             xb.at[tp, mine],
             a_send.at[i],
-            a_recv.at[mine],
-            dev_d(dx, dy),
-        )
+            a_recv.at[h, mine],
+            dev_d(dx, dy, dh),
+        )
+    send(xb.at[tp, pl.ds(8, 2)], xb.at[tp, pl.ds(8, 2)], k_sem.at[0], k_sem.at[1], h_other)
+    for load in loads:
+        load.start()
     row = lax.broadcasted_iota(jnp.int32, (128, FU), 0)
     col = lax.broadcasted_iota(jnp.int32, (128, FU), 1)
     place = ((col & 31) >> 3) * 28 + (col >> 5)
     spread[...] = jnp.where(row == place, 1.0, 0.0).astype(BF16)
-    own.wait()
-    for i, (dx, dy) in enumerate(dp_others):
-        g = lax.rem(x + dx, NX) * NY + lax.rem(y + dy, NY)
-        arrived(xb.at[tp, g], a_send.at[i], a_recv.at[g], dev_d(dx, dy))
-
     count = [0]
 
     def push(t, device):
@@ -189,15 +196,22 @@
 
     z1, z3, z2 = lax.rem(z + 1, NZ), lax.rem(z + 3, NZ), lax.rem(z + 2, NZ)
     hh = 1 - h
-    push(tp, h_other)
-    push(tp, z_next)
-    push(tp, z_prev)
-    push(tp, sib)
     across = t_of(hh, z, c)
-    here(across)
+    own.wait()
+    for there in range(2):
+        for i, (dx, dy, dh) in enumerate(row_others):
+            if dh == there:
+                g = lax.rem(x + dx, NX) * NY + lax.rem(y + dy, NY)
+                t = across if dh else tp
+                arrived(xb.at[t, g], a_send.at[i], a_recv.at[lax.rem(h + dh, NH), g], h_other)
+        if there == 0:
+            push(tp, sib)
+            push(tp, z_next)
+            push(tp, z_prev)
+    arrived(xb.at[across, pl.ds(8, 2)], k_sem.at[0], k_sem.at[1], h_other)
+    push(across, sib)
     push(across, z_next)
     push(across, z_prev)
-    push(across, sib)
 
     def gather_near():
         a, b = t_of(h, z1, c), t_of(h, z3, c)
@@ -432,6 +446,9 @@
     down(3)
     to_owners(3)
 
+    late = len(sent) - 7
+    for copy in sent[:late]:
+        copy.wait_send()
     for k in range(4):
         zz = lax.rem(z + OFFSETS[k], NZ)
         total = fsend[k, z * NY + h].astype(F32)
@@ -461,13 +478,13 @@
         arrived(crecv.at[g], c_send.at[i], c_recv.at[g], dev_d(dx, dy))
         total = total + crecv[g]
     rc_ref[...] = total[0, 0:64] / D
-    for copy in sent:
+    for copy in sent[late:]:
         copy.wait_send()
 
 
 def on_device(saved_input, keep_bits, norm_gain, gate_weight, up_weight, down_weight):
     vmem = pl.BlockSpec(memory_space=pltpu.VMEM)
-    hbm = pl.BlockSpec(memory_space=pl.ANY)
+    hbm = pl.BlockSpec(memory_space=pltpu.HBM)
     dma = pltpu.SemaphoreType.DMA
     out, check = pl.pallas_call(
         kernel,
@@ -475,7 +492,7 @@
             jax.ShapeDtypeStruct((64, DS), BF16),
             jax.ShapeDtypeStruct((64,), F32),
         ),
-        in_specs=[vmem, vmem, vmem, hbm, hbm, hbm],
+        in_specs=[hbm, vmem, vmem, hbm, hbm, hbm],
         out_specs=(vmem, vmem),
         scratch_shapes=[
             pltpu.VMEM((DS, FU), BF16),
@@ -483,6 +500,7 @@
             pltpu.VMEM((FU, DS), BF16),
             pltpu.VMEM((128, FU), BF16),
             pltpu.VMEM((8, 512), jnp.int32),
+            pltpu.VMEM((8, D), BF16),
             pltpu.VMEM((16, 10, 8, DS), BF16),
             pltpu.VMEM((256, DS), F32),
             pltpu.VMEM((4, 4, 2, 32, FU), BF16),
@@ -502,10 +520,11 @@
             pltpu.VMEM((8, 128), F32),
             pltpu.VMEM((8, 8, 128), F32),
             dma((3,)),
-            dma,
-            dma((7,)),
-            dma((8,)),
+            dma((2,)),
             dma((15,)),
+            dma((2, 8)),
+            dma((2,)),
+            dma((14,)),
             dma((16,)),
             dma((4, 7)),
             dma((4, 7)),
@@ -521,7 +540,7 @@
             dma((8,)),
         ],
         compiler_params=pltpu.CompilerParams(
-            collective_id=0, has_side_effects=True, vmem_limit_bytes=56 * 1024 * 1024
+            collective_id=0, has_side_effects=True, vmem_limit_bytes=54000 * 1024
         ),
         name="block",
     )(saved_input, keep_bits, norm_gain, gate_weight, up_weight, down_weight)

time: 84.7 us -> 82.7 us (0.976)
  Pallas kernels: 81.2 us -> 78.3 us
    pallas_call x1, Pallas kernels: 81.2 us -> 78.3 us  [on_device(): pl.pallas_call(kernel, out_shape=(jax.ShapeDtypeStruct((64, DS), BF16), j...]
    unnamed x2 -> x8, local copies, waits for them, and re-layouts: 2.74 us -> 3.46 us
where the time goes in v3:
time: 82.7 us; the launch traced here: 82.5 us
  Pallas kernels  78.3 us (95%)
  local copies, waits for them, and re-layouts  3.46 us (4%)
    pallas_call x1, Pallas kernels, on_device(): pl.pallas_call(kernel, out_shape=(jax.ShapeDtypeStruct((64, DS), BF16), j...  78.3 us
    unnamed x8, local copies, waits for them, and re-layouts  3.46 us

profile of v3, /device:TPU:1, one launch (start us, length us, event | category | flops | bytes accessed | tf_op | source)
XLA Modules:
  0.0 82.5 jit_solution(11960524608197425385)
XLA Ops:
  0.6 0.0 copy-start
  0.6 0.9 %copy-done = bf16[8,8192]{1,0:T(8,128)(2,1)S(1)} copy-done((bf16[8,8192]{1,0:T(8,128)(2,1)S(1)}, bf16[8,8192]{1,0:T(8,128)(2,1)}, u32[]{:S(2)}) %copy-start) | copy-done | bytes 131096
  1.5 0.0 copy-start.1
  1.5 0.7 copy-done.1
  2.3 0.0 copy-start.2
  2.3 0.7 copy-done.2
  2.9 78.3 %block.1 = (bf16[64,1024]{1,0:T(8,128)(2,1)S(1)}, f32[64]{0:T(128)S(1)}) custom-call(bf16[8,8192]{1,0:T(8,128)(2,1)S(1)} %copy-done, s32[8,448]{1,0:T(8,128)S(1)} %copy-done.1, bf16[1024]{0:T(1024)(128)(2,1)S(1)} %copy-done.2, bf16[1024,896]{1,0:T(8,128)(2,1)} %wg_hbm.1, bf16[1024,896]{1,0:T(8,128)(2,1)} %wu_hbm.1, bf16[896,1024]{1,0:T(8,128)(2,1)} %wd_hbm.1), custom_call_target="tpu_custom_call" | custom-call | tf_op jit(solution)/shard_map/block/pallas_call | solution.py:489
  81.3 0.7 copy.10
  81.9 0.5 copy.11
Async XLA Ops:
  0.6 0.9 %copy-start = (bf16[8,8192]{1,0:T(8,128)(2,1)S(1)}, bf16[8,8192]{1,0:T(8,128)(2,1)}, u32[]{:S(2)}) copy-start(bf16[8,8192]{1,0:T(8,128)(2,1)} %x_hbm.1) | copy-start | bytes 393220
  1.5 0.7 copy-start.1
  2.3 0.7 copy-start.2

commit v4 on v3

--- a/solution.py
+++ b/solution.py
@@ -17,8 +17,8 @@
 
 def kernel(
     x_hbm,
-    kb_ref,
-    gain_ref,
+    kb_hbm,
+    gain_hbm,
     wg_hbm,
     wu_hbm,
     wd_hbm,
@@ -29,6 +29,8 @@
     wd,
     spread,
     words,
+    kb_ref,
+    gain_ref,
     x_ref,
     xb,
     xn,
@@ -46,6 +48,8 @@
     orecv,
     fsend,
     frecv,
+    obuf,
+    sq,
     csend,
     crecv,
     w_sem,
@@ -124,8 +128,13 @@
         pltpu.make_async_copy(wg_hbm, wg, w_sem.at[1]),
         pltpu.make_async_copy(wd_hbm, wd, w_sem.at[2]),
     ]
-    rows_in = pltpu.make_async_copy(x_hbm, x_ref, l_sem.at[0])
-    rows_in.start()
+    rows_in = [
+        pltpu.make_async_copy(x_hbm, x_ref, l_sem.at[0]),
+        pltpu.make_async_copy(kb_hbm, kb_ref, l_sem.at[2]),
+        pltpu.make_async_copy(gain_hbm, gain_ref, l_sem.at[3]),
+    ]
+    for load in rows_in:
+        load.start()
     mine = x * NY + y
 
     barrier = pltpu.get_barrier_semaphore()
@@ -136,7 +145,8 @@
             continue
         pl.semaphore_signal(barrier, inc=1, device_id=dev_t(dh, dz), device_id_type=MESH)
     pl.semaphore_signal(barrier, inc=1, device_id=sib, device_id_type=MESH)
-    rows_in.wait()
+    for load in rows_in:
+        load.wait()
     own = pltpu.make_async_copy(
         x_ref.at[:, pl.ds(pl.multiple_of(dp * DS, DS), DS)], xb.at[tp, mine], l_sem.at[1]
     )
@@ -185,14 +195,17 @@
     col = lax.broadcasted_iota(jnp.int32, (128, FU), 1)
     place = ((col & 31) >> 3) * 28 + (col >> 5)
     spread[...] = jnp.where(row == place, 1.0, 0.0).astype(BF16)
-    count = [0]
-
-    def push(t, device):
-        send(xb.at[t], xb.at[t], x_send.at[count[0]], x_recv.at[t], device)
-        count[0] += 1
-
-    def here(t):
-        arrived(xb.at[t], x_send.at[0], x_recv.at[t], sib)
+    count = [0, 0]
+    xs, ks = pl.ds(0, 8), pl.ds(8, 2)
+
+    def push(t, device, part=0):
+        cells = xb.at[t, ks if part else xs]
+        send(cells, cells, x_send.at[part, count[part]], x_recv.at[part, t], device)
+        count[part] += 1
+
+    def here(t, part=0):
+        cells = xb.at[t, ks if part else xs]
+        arrived(cells, x_send.at[part, 0], x_recv.at[part, t], sib)
 
     z1, z3, z2 = lax.rem(z + 1, NZ), lax.rem(z + 3, NZ), lax.rem(z + 2, NZ)
     hh = 1 - h
@@ -208,58 +221,65 @@
             push(tp, sib)
             push(tp, z_next)
             push(tp, z_prev)
-    arrived(xb.at[across, pl.ds(8, 2)], k_sem.at[0], k_sem.at[1], h_other)
     push(across, sib)
     push(across, z_next)
     push(across, z_prev)
-
-    def gather_near():
+    push(tp, sib, 1)
+    push(tp, z_next, 1)
+    push(tp, z_prev, 1)
+    arrived(xb.at[across, ks], k_sem.at[0], k_sem.at[1], h_other)
+    push(across, sib, 1)
+    push(across, z_next, 1)
+    push(across, z_prev, 1)
+
+    def gather_near(part):
         a, b = t_of(h, z1, c), t_of(h, z3, c)
         e, f = t_of(hh, z1, c), t_of(hh, z3, c)
-        here(a)
-        push(a, z_prev)
-        push(a, sib)
-        here(b)
-        push(b, sib)
-        here(f)
-        push(f, z_next)
-        push(f, sib)
-        here(e)
-        push(e, sib)
-
-    def gather_far():
+        here(a, part)
+        push(a, z_prev, part)
+        push(a, sib, part)
+        here(b, part)
+        push(b, sib, part)
+        here(f, part)
+        push(f, z_next, part)
+        push(f, sib, part)
+        here(e, part)
+        push(e, sib, part)
+
+    def gather_far(part):
         a, b = t_of(h, z2, c), t_of(hh, z2, c)
-        here(a)
-        push(a, sib)
-        here(b)
-        push(b, sib)
+        here(a, part)
+        push(a, sib, part)
+        here(b, part)
+        push(b, sib, part)
+
+    def source(k):
+        return 1 - c if k % 2 == 0 else c, lax.rem(z + OFFSETS[k // 2], NZ)
 
     xn1, xp1, xf = lax.rem(x + 1, NX), lax.rem(x + 3, NX), lax.rem(x + 2, NX)
 
     def matmul(k):
-        zz = lax.rem(z + OFFSETS[k], NZ)
-        here(t_of(0, zz, 1 - c))
-        here(t_of(1, zz, 1 - c))
-        blocks = [t_of(a, zz, b) for a in range(2) for b in range(2)]
+        hs, zz = source(k)
+        here(t_of(hs, zz, 1 - c))
         gain = gain_ref[...].astype(F32).reshape(1, DS)
         for g in range(8):
-            for i in range(4):
-                v = xb[blocks[i], g].astype(F32) * gain
-                xn[pl.ds(g * 32 + i * 8, 8), :] = v
+            for i in range(2):
+                v = xb[t_of(hs, zz, i), g].astype(F32) * gain
+                xn[pl.ds(g * 16 + i * 8, 8), :] = v
         lhs = xn[...].astype(BF16)
         if k == 0:
             loads[0].wait()
-        acc = jnp.dot(lhs, wu[...], preferred_element_type=F32).astype(BF16)
+        acc = jnp.dot(lhs, wu[...], preferred_element_type=F32)
         for g in range(8):
             for i in range(2):
-                lo = g * 32 + i * 16
-                pu[k, g % 2, g // 2, i] = acc[lo : lo + 16]
+                lo = g * 16 + i * 8
+                pu[k, g % 2, g // 2, i] = acc[lo : lo + 8].astype(BF16)
         send(pu.at[k, 1 - y], u_y.at[k], u_send.at[k, 0], u_done.at[k, 0], y_other)
         if k == 0:
             loads[1].wait()
         acc = jnp.dot(lhs, wg[...], preferred_element_type=F32).astype(BF16)
         for g in range(8):
-            pg[k, g // 2, g % 2] = acc[g * 32 : g * 32 + 32]
+            pg[k, g // 2, g % 2] = acc[g * 16 : g * 16 + 16]
         send(pg.at[k, xf, 0], g_relay.at[k, 0], g_send.at[k, 0], g_done.at[k, 0], x_next)
         send(pg.at[k, xf, 1], g_relay.at[k, 1], g_send.at[k, 1], g_done.at[k, 1], x_prev)
         send(pg.at[k, xn1, 1], g_recv.at[k, 0, 1], g_send.at[k, 3], g_done.at[k, 3], x_next)
@@ -316,22 +336,17 @@
         send(pu.at[k, y, xp1, 1], u_recv.at[k, 1, 1], u_send.at[k, 6], u_done.at[k, 6], x_prev)
 
     def hidden(k):
-        zz = lax.rem(z + OFFSETS[k], NZ)
+        hs, zz = source(k)
+        here(t_of(hs, zz, 1 - c), 1)
         lanes = pl.ds(pl.multiple_of(lax.rem(tp, 8) * 128, 128), 128)
-        slots = jnp.concatenate(
-            [
-                xb[t_of(a, zz, b), 8 + lax.div(tp, 8), :, lanes].astype(F32)
-                for a in range(2)
-                for b in range(2)
-            ],
-            axis=0,
-        )
-        lane = lax.broadcasted_iota(jnp.int32, (32, 128), 1)
+        slots = [xb[t_of(hs, zz, i), 8 + lax.div(tp, 8), :, lanes].astype(F32) for i in range(2)]
+        slots = jnp.concatenate(slots, axis=0)
+        lane = lax.broadcasted_iota(jnp.int32, (16, 128), 1)
         inv = jnp.sum(
             jnp.where((lane >= 112) & (lane < 115), slots, 0.0), axis=1, keepdims=True
         )
         byte = jnp.dot(slots.astype(BF16), spread[...], preferred_element_type=F32)
-        unit = lax.broadcasted_iota(jnp.int32, (32, FU), 1)
+        unit = lax.broadcasted_iota(jnp.int32, (16, FU), 1)
         bit = (byte.astype(jnp.int32) >> (unit & 7)) & 1
         keep = 2.0 * bit.astype(F32)
         arrived(yrecv.at[k], g_send.at[k, 6], g_done.at[k, 6], y_other)
@@ -341,7 +356,7 @@
         arrived(u_recv.at[k, 0, 0], u_send.at[k, 5], u_done.at[k, 5], x_next)
         arrived(u_recv.at[k, 1, 1], u_send.at[k, 6], u_done.at[k, 6], x_prev)
         up = pu[k, y, x].astype(F32) + u_recv[k, 0].astype(F32) + u_recv[k, 1].astype(F32)
-        up = up.reshape(32, FU) * inv
+        up = up.reshape(16, FU) * inv
         hid[k, x, y] = (gate / (1.0 + jnp.exp(-gate)) * up * keep).astype(BF16)
         for i, device in enumerate((x_next, x_prev, y_other)):
             send(hid.at[k, x, y], hid.at[k, x, y], h_send.at[k, i], h_recv.at[k, mine], device)
@@ -381,70 +396,100 @@
         h_here(k, xf, 1)
         if k == 0:
             loads[2].wait()
-        lhs = hid[k].reshape(256, FU)
-        acc = jnp.dot(lhs, wd[...], preferred_element_type=F32).astype(BF16)
-        for g in range(8):
-            for s in range(2):
-                osum[k, s, g] = acc[g * 32 + s * 16 : g * 32 + s * 16 + 16]
-        send(osum.at[k, 1 - c], orecv.at[k], o_send.at[k], o_recv.at[k], sib)
-
-    def to_owners(k):
-        zz = lax.rem(z + OFFSETS[k], NZ)
-        arrived(orecv.at[k], o_send.at[k], o_recv.at[k], sib)
-        fsend[k] = (osum[k, c].astype(F32) + orecv[k].astype(F32)).astype(BF16)
-        here_index = h * NZ + z
-        for i, (dh, dz) in enumerate(tp_others):
-            g = lax.rem(z + dz, NZ) * NY + lax.rem(h + dh, NH)
+        acc = jnp.dot(hid[k].reshape(128, FU), wd[...], preferred_element_type=F32)
+        i = k // 2
+        if k % 2 == 0:
+            osum[i] = acc.astype(BF16).reshape(8, 16, DS)
+            send(osum.at[i], orecv.at[i], o_send.at[i], o_recv.at[i], sib)
+            return
+        _, zz = source(k)
+        arrived(orecv.at[i], o_send.at[i], o_recv.at[i], sib)
+        fsend[i] = (acc.reshape(8, 16, DS) + orecv[i].astype(F32)).astype(BF16)
+        for j, (dh, dz) in enumerate(tp_others):
             send(
-                fsend.at[k, g],
-                frecv.at[here_index, zz],
-                f_send.at[k, i],
-                f_recv.at[here_index, zz],
+                fsend.at[i, lax.rem(z + dz, NZ) * NY + lax.rem(h + dh, NH)],
+                frecv.at[h * NZ + z, zz],
+                f_send.at[i, j],
+                f_recv.at[h * NZ + z, zz],
                 dev_t(dh, dz),
             )
 
     matmul(0)
-    gather_near()
+    matmul(1)
     gate_relay(0)
-    matmul(2)
-    matmul(1)
+    up_over_y(0)
+    gate_relay(1)
+    gather_near(0)
     gate_y(0)
-    up_over_y(0)
-    gather_far()
-    matmul(3)
-    up_over_y(2)
-    gate_relay(3)
     up_relay(0)
     up_over_y(1)
-    gate_relay(1)
+    matmul(2)
+    matmul(3)
+    gate_y(1)
+    up_relay(1)
+    matmul(4)
+    hidden(0)
+    up_over_y(2)
+    matmul(5)
     gate_relay(2)
-    hidden(0)
-    up_relay(1)
+    gate_relay(3)
+    gather_near(1)
     up_relay(2)
-    gate_y(1)
+    gate_relay(5)
+    gate_relay(4)
+    up_over_y(3)
+    gather_far(0)
+    up_over_y(4)
     gate_y(2)
-    up_over_y(3)
-    gate_y(3)
     pass_y(0)
     hidden(1)
+    matmul(6)
+    up_relay(3)
+    up_over_y(5)
+    gate_y(4)
+    pass_x(0)
+    gate_y(3)
+    pass_y(1)
+    up_relay(4)
+    gate_y(5)
     hidden(2)
-    pass_x(0)
-    pass_y(1)
-    up_relay(3)
-    pass_y(2)
+    gate_relay(6)
+    up_relay(5)
+    gather_far(1)
+    matmul(7)
     down(0)
     pass_x(1)
+    up_over_y(6)
     hidden(3)
+    gate_relay(7)
+    pass_y(2)
+    hidden(4)
+    hidden(5)
+    up_over_y(7)
+    pass_y(3)
+    gate_y(6)
+    up_relay(6)
+    down(1)
+    gate_y(7)
     pass_x(2)
-    to_owners(0)
-    down(1)
-    pass_y(3)
-    to_owners(1)
+    pass_y(4)
+    up_relay(7)
+    pass_x(3)
+    pass_y(5)
+    hidden(6)
     down(2)
-    pass_x(3)
-    to_owners(2)
+    pass_x(4)
+    hidden(7)
     down(3)
-    to_owners(3)
+    pass_y(6)
+    pass_x(5)
+    pass_y(7)
+    down(4)
+    pass_x(6)
+    down(5)
+    pass_x(7)
+    down(6)
+    down(7)
 
     late = len(sent) - 7
     for copy in sent[:late]:
@@ -461,13 +506,17 @@
             arrived(frecv.at[src, zz], f_send.at[0, i], f_recv.at[src, zz], dev_t(dh, dz))
             total = total + frecv[src, zz].astype(F32)
         rounded = total.astype(BF16)
-        out_ref[pl.ds(pl.multiple_of(zz * 16, 16), 16), :] = rounded
-    wide = out_ref[...].astype(F32)
-    wide = wide * wide
-    folded = wide[:, 0:128]
-    for i in range(1, 8):
-        folded = folded + wide[:, i * 128 : (i + 1) * 128]
-    rowsum = jnp.sum(folded.T, axis=0, keepdims=True)
+        rows = pl.ds(pl.multiple_of(zz * 16, 16), 16)
+        obuf[rows, :] = rounded
+        wide = rounded.astype(F32)
+        wide = wide * wide
+        folded = wide[:, 0:128]
+        for i in range(1, 8):
+            folded = folded + wide[:, i * 128 : (i + 1) * 128]
+        sq[rows, :] = folded
+    result = pltpu.make_async_copy(obuf, out_ref, l_sem.at[0])
+    result.start()
+    rowsum = jnp.sum(sq[...].T, axis=0, keepdims=True)
     csend[:, 0:64] = jnp.broadcast_to(rowsum, (8, 64))
     csend[:, 64:128] = jnp.zeros((8, 64), F32)
     for i, (dx, dy) in enumerate(dp_others):
@@ -478,6 +527,7 @@
         arrived(crecv.at[g], c_send.at[i], c_recv.at[g], dev_d(dx, dy))
         total = total + crecv[g]
     rc_ref[...] = total[0, 0:64] / D
+    result.wait()
     for copy in sent[late:]:
         copy.wait_send()
 
@@ -492,46 +542,50 @@
             jax.ShapeDtypeStruct((64, DS), BF16),
             jax.ShapeDtypeStruct((64,), F32),
         ),
-        in_specs=[hbm, vmem, vmem, hbm, hbm, hbm],
-        out_specs=(vmem, vmem),
+        in_specs=[hbm] * 6,
+        out_specs=(hbm, vmem),
         scratch_shapes=[
             pltpu.VMEM((DS, FU), BF16),
             pltpu.VMEM((DS, FU), BF16),
             pltpu.VMEM((FU, DS), BF16),
             pltpu.VMEM((128, FU), BF16),
             pltpu.VMEM((8, 512), jnp.int32),
+            pltpu.VMEM((8, 448), jnp.int32),
+            pltpu.VMEM((DS,), BF16),
             pltpu.VMEM((8, D), BF16),
             pltpu.VMEM((16, 10, 8, DS), BF16),
-            pltpu.VMEM((256, DS), F32),
-            pltpu.VMEM((4, 4, 2, 32, FU), BF16),
-            pltpu.VMEM((4, 2, 4, 2, 16, FU), BF16),
-            pltpu.VMEM((4, 2, 32, FU), BF16),
-            pltpu.VMEM((4, 2, 2, 32, FU), BF16),
-            pltpu.VMEM((4, 2, 16, FU), BF16),
-            pltpu.VMEM((4, 2, 2, 16, FU), BF16),
-            pltpu.VMEM((4, 4, 2, 16, FU), BF16),
-            pltpu.VMEM((4, 32, FU), BF16),
-            pltpu.VMEM((4, 32, FU), BF16),
-            pltpu.VMEM((4, 4, 2, 32, FU), BF16),
-            pltpu.VMEM((4, 2, 8, 16, DS), BF16),
+            pltpu.VMEM((128, DS), F32),
+            pltpu.VMEM((8, 4, 2, 16, FU), BF16),
+            pltpu.VMEM((8, 2, 4, 2, 8, FU), BF16),
+            pltpu.VMEM((8, 2, 16, FU), BF16),
+            pltpu.VMEM((8, 2, 2, 16, FU), BF16),
+            pltpu.VMEM((8, 2, 8, FU), BF16),
+            pltpu.VMEM((8, 2, 2, 8, FU), BF16),
+            pltpu.VMEM((8, 4, 2, 8, FU), BF16),
+            pltpu.VMEM((8, 16, FU), BF16),
+            pltpu.VMEM((8, 16, FU), BF16),
+            pltpu.VMEM((8, 4, 2, 16, FU), BF16),
+            pltpu.VMEM((4, 8, 16, DS), BF16),
             pltpu.VMEM((4, 8, 16, DS), BF16),
             pltpu.VMEM((4, 8, 16, DS), BF16),
             pltpu.VMEM((8, 4, 16, DS), BF16),
+            pltpu.VMEM((64, DS), BF16),
+            pltpu.VMEM((64, 128), F32),
             pltpu.VMEM((8, 128), F32),
             pltpu.VMEM((8, 8, 128), F32),
             dma((3,)),
-            dma((2,)),
+            dma((4,)),
             dma((15,)),
             dma((2, 8)),
             dma((2,)),
-            dma((14,)),
-            dma((16,)),
-            dma((4, 7)),
-            dma((4, 7)),
-            dma((4, 7)),
-            dma((4, 7)),
-            dma((4, 7)),
-            dma((4, 8)),
+            dma((2, 14)),
+            dma((2, 16)),
+            dma((8, 7)),
+            dma((8, 7)),
+            dma((8, 7)),
+            dma((8, 7)),
+            dma((8, 7)),
+            dma((8, 8)),
             dma((4,)),
             dma((4,)),
             dma((4, 7)),
@@ -540,7 +594,7 @@
             dma((8,)),
         ],
         compiler_params=pltpu.CompilerParams(
-            collective_id=0, has_side_effects=True, vmem_limit_bytes=54000 * 1024
+            collective_id=0, has_side_effects=True, vmem_limit_bytes=56 * 1024 * 1024
         ),
         name="block",
     )(saved_input, keep_bits, norm_gain, gate_weight, up_weight, down_weight)

time: 82.7 us -> 83.1 us (level)
  Pallas kernels: 78.3 us -> 79.5 us
    pallas_call x1, Pallas kernels: 78.3 us -> 79.5 us  [on_device(): pl.pallas_call(kernel, out_shape=(jax.ShapeDtypeStruct((64, DS), BF16), j...]
    unnamed x8 -> x2, local copies, waits for them, and re-layouts: 3.46 us -> 2.74 us
where the time goes in v4:
time: 83.1 us; the launch traced here: 82.8 us
  Pallas kernels  79.5 us (96%)
  local copies, waits for them, and re-layouts  2.74 us (3%)
    pallas_call x1, Pallas kernels, on_device(): pl.pallas_call(kernel, out_shape=(jax.ShapeDtypeStruct((64, DS), BF16), j...  79.5 us
    unnamed x2, local copies, waits for them, and re-layouts  2.74 us

profile of v4, /device:TPU:1, one launch (start us, length us, event | category | flops | bytes accessed | tf_op | source)
XLA Modules:
  0.0 82.8 jit_solution(5043807074314232279)
XLA Ops:
  0.6 79.5 %block.1 = (bf16[64,1024]{1,0:T(8,128)(2,1)}, f32[64]{0:T(128)}) custom-call(bf16[8,8192]{1,0:T(8,128)(2,1)} %x_hbm.1, s32[8,448]{1,0:T(8,128)} %kb_hbm.1, bf16[1024]{0:T(1024)(128)(2,1)} %gain_hbm.1, bf16[1024,896]{1,0:T(8,128)(2,1)} %wg_hbm.1, bf16[1024,896]{1,0:T(8,128)(2,1)} %wu_hbm.1, bf16[896,1024]{1,0:T(8,128)(2,1)} %wd_hbm.1), custom_call_target="tpu_custom_call" | custom-call | tf_op jit(solution)/shard_map/block/pallas_call | solution.py:539
  80.1 1.6 %copy.10 = bf16[64,1024]{1,0:T(8,128)(2,1)} copy(bf16[64,1024]{1,0:T(8,128)(2,1)} %get-tuple-element.4) | data formatting | bytes 262144
  81.7 1.2 %copy.11 = f32[64]{0:T(128)} copy(f32[64]{0:T(128)} %get-tuple-element.5) | data formatting | bytes 512

commit v5 on v4

--- a/solution.py
+++ b/solution.py
@@ -59,12 +59,13 @@
     k_sem,
     x_send,
     x_recv,
+    k_recv,
     g_send,
     g_done,
     u_send,
     u_done,
     h_send,
-    h_recv,
+    h_done,
     o_send,
     o_recv,
     f_send,
@@ -93,7 +94,6 @@
     sib = dev_t(0, 0, 1)
     h_other = dev_t(1, 0)
     z_next, z_prev = dev_t(0, 1), dev_t(0, NZ - 1)
-    sent = []
 
     def send(src, dst, ssem, rsem, device):
         copy = pltpu.make_async_remote_copy(
@@ -105,17 +105,26 @@
             device_id_type=MESH,
         )
         copy.start()
-        sent.append(copy)
-
-    def arrived(dst, ssem, rsem, device):
+
+    def arrived(dst, rsem, device):
         pltpu.make_async_remote_copy(
             src_ref=dst,
             dst_ref=dst,
-            send_sem=ssem,
+            send_sem=rsem,
             recv_sem=rsem,
             device_id=device,
             device_id_type=MESH,
         ).wait_recv()
+
+    def left(src, ssem, device):
+        pltpu.make_async_remote_copy(
+            src_ref=src,
+            dst_ref=src,
+            send_sem=ssem,
+            recv_sem=ssem,
+            device_id=device,
+            device_id_type=MESH,
+        ).wait_send()
 
     dp_others = [(dx, dy) for dx in (1, 3, 2, 0) for dy in (0, 1) if (dx, dy) != (0, 0)]
     tp_others = [(dh, dz) for dz in (2, 1, 3, 0) for dh in (1, 0) if (dh, dz) != (0, 0)]
@@ -179,13 +188,13 @@
         xb[tp, 8 + t // 8, :, (t % 8) * 128 : (t % 8) * 128 + 128] = slot
     pl.semaphore_wait(barrier, len(row_others) + 7)
 
-    for i, (dx, dy, dh) in enumerate(row_others):
+    for dx, dy, dh in row_others:
         there = lax.rem(y + dy, NY) * NX + lax.rem(x + dx, NX)
         send(
             x_ref.at[:, pl.ds(pl.multiple_of(there * DS, DS), DS)],
             xb.at[tp, mine],
-            a_send.at[i],
-            a_recv.at[h, mine],
+            a_send.at[dh],
+            a_recv.at[dh],
             dev_d(dx, dy, dh),
         )
     send(xb.at[tp, pl.ds(8, 2)], xb.at[tp, pl.ds(8, 2)], k_sem.at[0], k_sem.at[1], h_other)
@@ -195,63 +204,56 @@
     col = lax.broadcasted_iota(jnp.int32, (128, FU), 1)
     place = ((col & 31) >> 3) * 28 + (col >> 5)
     spread[...] = jnp.where(row == place, 1.0, 0.0).astype(BF16)
-    count = [0, 0]
     xs, ks = pl.ds(0, 8), pl.ds(8, 2)
 
-    def push(t, device, part=0):
+    def push(t, device, part, rsem):
         cells = xb.at[t, ks if part else xs]
-        send(cells, cells, x_send.at[part, count[part]], x_recv.at[part, t], device)
-        count[part] += 1
-
-    def here(t, part=0):
-        cells = xb.at[t, ks if part else xs]
-        arrived(cells, x_send.at[part, 0], x_recv.at[part, t], sib)
+        send(cells, cells, x_send.at[part], rsem, device)
+
+    def here(t):
+        arrived(xb.at[t, xs], x_recv.at[t], sib)
+
+    def push_x(t, *devices):
+        for device in devices:
+            push(t, device, 0, x_recv.at[t])
 
     z1, z3, z2 = lax.rem(z + 1, NZ), lax.rem(z + 3, NZ), lax.rem(z + 2, NZ)
     hh = 1 - h
     across = t_of(hh, z, c)
     own.wait()
     for there in range(2):
-        for i, (dx, dy, dh) in enumerate(row_others):
-            if dh == there:
-                g = lax.rem(x + dx, NX) * NY + lax.rem(y + dy, NY)
-                t = across if dh else tp
-                arrived(xb.at[t, g], a_send.at[i], a_recv.at[lax.rem(h + dh, NH), g], h_other)
         if there == 0:
-            push(tp, sib)
-            push(tp, z_next)
-            push(tp, z_prev)
-    push(across, sib)
-    push(across, z_next)
-    push(across, z_prev)
-    push(tp, sib, 1)
-    push(tp, z_next, 1)
-    push(tp, z_prev, 1)
-    arrived(xb.at[across, ks], k_sem.at[0], k_sem.at[1], h_other)
-    push(across, sib, 1)
-    push(across, z_next, 1)
-    push(across, z_prev, 1)
+            arrived(xb.at[tp, pl.ds(0, 7)], a_recv.at[0], y_other)
+        else:
+            arrived(xb.at[across, pl.ds(0, 8)], a_recv.at[1], h_other)
+        push_x(across if there else tp, sib, z_next, z_prev)
+    for t in (tp, across):
+        if t is across:
+            arrived(xb.at[across, ks], k_sem.at[1], h_other)
+        push(t, sib, 1, k_recv.at[0])
+        push(t, z_next, 1, k_recv.at[1])
+        push(t, z_prev, 1, k_recv.at[1])
+
+    near = [t_of(h, z1, c), t_of(h, z3, c), t_of(hh, z3, c), t_of(hh, z1, c)]
+    distant = [t_of(h, z2, c), t_of(hh, z2, c)]
 
     def gather_near(part):
-        a, b = t_of(h, z1, c), t_of(h, z3, c)
-        e, f = t_of(hh, z1, c), t_of(hh, z3, c)
-        here(a, part)
-        push(a, z_prev, part)
-        push(a, sib, part)
-        here(b, part)
-        push(b, sib, part)
-        here(f, part)
-        push(f, z_next, part)
-        push(f, sib, part)
-        here(e, part)
-        push(e, sib, part)
+        if part:
+            arrived(xb.at[pl.ds(0, 4), ks], k_recv.at[1], z_next)
+        for i, t in enumerate(near):
+            if not part:
+                here(t)
+            if i in (0, 2):
+                push(t, z_prev if i == 0 else z_next, part, k_recv.at[2] if part else x_recv.at[t])
+            push(t, sib, part, k_recv.at[3] if part else x_recv.at[t])
 
     def gather_far(part):
-        a, b = t_of(h, z2, c), t_of(hh, z2, c)
-        here(a, part)
-        push(a, sib, part)
-        here(b, part)
-        push(b, sib, part)
+        if part:
+            arrived(xb.at[pl.ds(0, 2), ks], k_recv.at[2], z_next)
+        for t in distant:
+            if not part:
+                here(t)
+            push(t, sib, part, k_recv.at[4] if part else x_recv.at[t])
 
     def source(k):
         return 1 - c if k % 2 == 0 else c, lax.rem(z + OFFSETS[k // 2], NZ)
@@ -274,26 +276,25 @@
             for i in range(2):
                 lo = g * 16 + i * 8
                 pu[k, g % 2, g // 2, i] = acc[lo : lo + 8].astype(BF16)
-        send(pu.at[k, 1 - y], u_y.at[k], u_send.at[k, 0], u_done.at[k, 0], y_other)
+        send(pu.at[k, 1 - y], u_y.at[k], u_send, u_done.at[k, 0], y_other)
         if k == 0:
             loads[1].wait()
         acc = jnp.dot(lhs, wg[...], preferred_element_type=F32).astype(BF16)
         for g in range(8):
             pg[k, g // 2, g % 2] = acc[g * 16 : g * 16 + 16]
-        send(pg.at[k, xf, 0], g_relay.at[k, 0], g_send.at[k, 0], g_done.at[k, 0], x_next)
-        send(pg.at[k, xf, 1], g_relay.at[k, 1], g_send.at[k, 1], g_done.at[k, 1], x_prev)
-        send(pg.at[k, xn1, 1], g_recv.at[k, 0, 1], g_send.at[k, 3], g_done.at[k, 3], x_next)
-        send(pg.at[k, xp1, 0], g_recv.at[k, 1, 0], g_send.at[k, 4], g_done.at[k, 4], x_prev)
+        send(pg.at[k, xf, 0], g_relay.at[k, 0], g_send, g_done.at[k, 0], x_next)
+        send(pg.at[k, xf, 1], g_relay.at[k, 1], g_send, g_done.at[k, 0], x_prev)
+        send(pg.at[k, xn1, 1], g_recv.at[k, 0, 1], g_send, g_done.at[k, 1], x_next)
+        send(pg.at[k, xp1, 0], g_recv.at[k, 1, 0], g_send, g_done.at[k, 1], x_prev)
 
     def gate_relay(k):
-        arrived(g_relay.at[k, 0], g_send.at[k, 0], g_done.at[k, 0], x_next)
+        arrived(g_relay.at[k], g_done.at[k, 0], x_next)
         v = pg[k, xn1, 0].astype(F32) + g_relay[k, 0].astype(F32)
         pg[k, xn1, 0] = v.astype(BF16)
-        send(pg.at[k, xn1, 0], g_recv.at[k, 0, 0], g_send.at[k, 2], g_done.at[k, 2], x_next)
-        arrived(g_relay.at[k, 1], g_send.at[k, 1], g_done.at[k, 1], x_prev)
+        send(pg.at[k, xn1, 0], g_recv.at[k, 0, 0], g_send, g_done.at[k, 1], x_next)
         v = pg[k, xp1, 1].astype(F32) + g_relay[k, 1].astype(F32)
         pg[k, xp1, 1] = v.astype(BF16)
-        send(pg.at[k, xp1, 1], g_recv.at[k, 1, 1], g_send.at[k, 5], g_done.at[k, 5], x_prev)
+        send(pg.at[k, xp1, 1], g_recv.at[k, 1, 1], g_send, g_done.at[k, 1], x_prev)
 
     def gate_over_x(k, yy):
         return (
@@ -301,43 +302,41 @@
         )
 
     def gate_y(k):
-        arrived(g_recv.at[k, 0, 1], g_send.at[k, 3], g_done.at[k, 3], x_next)
-        arrived(g_recv.at[k, 1, 0], g_send.at[k, 4], g_done.at[k, 4], x_prev)
-        arrived(g_recv.at[k, 0, 0], g_send.at[k, 2], g_done.at[k, 2], x_next)
-        arrived(g_recv.at[k, 1, 1], g_send.at[k, 5], g_done.at[k, 5], x_prev)
+        arrived(g_recv.at[k], g_done.at[k, 1], x_next)
         ysend[k] = gate_over_x(k, 1 - y).astype(BF16)
-        send(ysend.at[k], yrecv.at[k], g_send.at[k, 6], g_done.at[k, 6], y_other)
+        send(ysend.at[k], yrecv.at[k], g_send, g_done.at[k, 2], y_other)
 
     def up_over_y(k):
-        arrived(u_y.at[k], u_send.at[k, 0], u_done.at[k, 0], y_other)
+        arrived(u_y.at[k], u_done.at[k, 0], y_other)
         for xx in (xf, xn1, xp1, x):
             v = pu[k, y, xx].astype(F32) + u_y[k, xx].astype(F32)
             pu[k, y, xx] = v.astype(BF16)
             if xx is xf:
-                send(pu.at[k, y, xf, 0], u_relay.at[k, 0], u_send.at[k, 1], u_done.at[k, 1], x_next)
-                send(pu.at[k, y, xf, 1], u_relay.at[k, 1], u_send.at[k, 2], u_done.at[k, 2], x_prev)
+                send(pu.at[k, y, xf, 0], u_relay.at[k, 0], u_send, u_done.at[k, 1], x_next)
+                send(pu.at[k, y, xf, 1], u_relay.at[k, 1], u_send, u_done.at[k, 1], x_prev)
             if xx is xn1:
                 send(
-                    pu.at[k, y, xx, 1], u_recv.at[k, 0, 1], u_send.at[k, 3], u_done.at[k, 3], x_next
+                    pu.at[k, y, xx, 1], u_recv.at[k, 0, 1], u_send, u_done.at[k, 2], x_next
                 )
             if xx is xp1:
                 send(
-                    pu.at[k, y, xx, 0], u_recv.at[k, 1, 0], u_send.at[k, 4], u_done.at[k, 4], x_prev
+                    pu.at[k, y, xx, 0], u_recv.at[k, 1, 0], u_send, u_done.at[k, 2], x_prev
                 )
 
     def up_relay(k):
-        arrived(u_relay.at[k, 0], u_send.at[k, 1], u_done.at[k, 1], x_next)
+        arrived(u_relay.at[k], u_done.at[k, 1], x_next)
         v = pu[k, y, xn1, 0].astype(F32) + u_relay[k, 0].astype(F32)
         pu[k, y, xn1, 0] = v.astype(BF16)
-        send(pu.at[k, y, xn1, 0], u_recv.at[k, 0, 0], u_send.at[k, 5], u_done.at[k, 5], x_next)
-        arrived(u_relay.at[k, 1], u_send.at[k, 2], u_done.at[k, 2], x_prev)
+        send(pu.at[k, y, xn1, 0], u_recv.at[k, 0, 0], u_send, u_done.at[k, 2], x_next)
         v = pu[k, y, xp1, 1].astype(F32) + u_relay[k, 1].astype(F32)
         pu[k, y, xp1, 1] = v.astype(BF16)
-        send(pu.at[k, y, xp1, 1], u_recv.at[k, 1, 1], u_send.at[k, 6], u_done.at[k, 6], x_prev)
+        send(pu.at[k, y, xp1, 1], u_recv.at[k, 1, 1], u_send, u_done.at[k, 2], x_prev)
 
     def hidden(k):
         hs, zz = source(k)
-        here(t_of(hs, zz, 1 - c), 1)
+        if k in (0, 2, 6):
+            blocks, i = {0: (2, 0), 2: (4, 3), 6: (2, 4)}[k]
+            arrived(xb.at[pl.ds(0, blocks), ks], k_recv.at[i], sib)
         lanes = pl.ds(pl.multiple_of(lax.rem(tp, 8) * 128, 128), 128)
         slots = [xb[t_of(hs, zz, i), 8 + lax.div(tp, 8), :, lanes].astype(F32) for i in range(2)]
         slots = jnp.concatenate(slots, axis=0)
@@ -349,68 +348,51 @@
         unit = lax.broadcasted_iota(jnp.int32, (16, FU), 1)
         bit = (byte.astype(jnp.int32) >> (unit & 7)) & 1
         keep = 2.0 * bit.astype(F32)
-        arrived(yrecv.at[k], g_send.at[k, 6], g_done.at[k, 6], y_other)
+        arrived(yrecv.at[k], g_done.at[k, 2], y_other)
         gate = (gate_over_x(k, y) + yrecv[k].astype(F32)) * inv
-        arrived(u_recv.at[k, 0, 1], u_send.at[k, 3], u_done.at[k, 3], x_next)
-        arrived(u_recv.at[k, 1, 0], u_send.at[k, 4], u_done.at[k, 4], x_prev)
-        arrived(u_recv.at[k, 0, 0], u_send.at[k, 5], u_done.at[k, 5], x_next)
-        arrived(u_recv.at[k, 1, 1], u_send.at[k, 6], u_done.at[k, 6], x_prev)
+        arrived(u_recv.at[k], u_done.at[k, 2], x_next)
         up = pu[k, y, x].astype(F32) + u_recv[k, 0].astype(F32) + u_recv[k, 1].astype(F32)
         up = up.reshape(16, FU) * inv
         hid[k, x, y] = (gate / (1.0 + jnp.exp(-gate)) * up * keep).astype(BF16)
-        for i, device in enumerate((x_next, x_prev, y_other)):
-            send(hid.at[k, x, y], hid.at[k, x, y], h_send.at[k, i], h_recv.at[k, mine], device)
-
-    def h_here(k, xx, yy):
-        arrived(hid.at[k, xx, yy], h_send.at[k, 0], h_recv.at[k, xx * NY + yy], x_next)
+        near_y, far_y = 1 + y, 2 - y
+        block = hid.at[k, x, y]
+        send(block, block, h_send, h_done.at[k, 0], y_other)
+        send(block, block, h_send, h_done.at[k, near_y], x_next)
+        send(block, block, h_send, h_done.at[k, far_y], x_prev)
 
     def pass_y(k):
-        h_here(k, x, 1 - y)
-        for i, device in enumerate((x_next, x_prev)):
-            send(
-                hid.at[k, x, 1 - y],
-                hid.at[k, x, 1 - y],
-                h_send.at[k, 3 + i],
-                h_recv.at[k, x * NY + 1 - y],
-                device,
-            )
+        block = hid.at[k, x, 1 - y]
+        arrived(block, h_done.at[k, 0], y_other)
+        near_y, far_y = 1 + y, 2 - y
+        send(block, block, h_send, h_done.at[k, far_y], x_next)
+        send(block, block, h_send, h_done.at[k, near_y], x_prev)
 
     def pass_x(k):
-        h_here(k, xp1, 0)
-        send(
-            hid.at[k, xp1, 0], hid.at[k, xp1, 0], h_send.at[k, 5], h_recv.at[k, xp1 * NY], x_next
-        )
-        h_here(k, xn1, 1)
-        send(
-            hid.at[k, xn1, 1],
-            hid.at[k, xn1, 1],
-            h_send.at[k, 6],
-            h_recv.at[k, xn1 * NY + 1],
-            x_prev,
-        )
+        arrived(hid.at[k, 0], h_done.at[k, 1], x_next)
+        block = hid.at[k, xp1, 0]
+        send(block, block, h_send, h_done.at[k, 2], x_next)
+        block = hid.at[k, xn1, 1]
+        send(block, block, h_send, h_done.at[k, 2], x_prev)
 
     def down(k):
-        h_here(k, xp1, 1)
-        h_here(k, xn1, 0)
-        h_here(k, xf, 0)
-        h_here(k, xf, 1)
+        arrived(hid.at[k, pl.ds(0, 2)], h_done.at[k, 2], x_next)
         if k == 0:
             loads[2].wait()
         acc = jnp.dot(hid[k].reshape(128, FU), wd[...], preferred_element_type=F32)
         i = k // 2
         if k % 2 == 0:
             osum[i] = acc.astype(BF16).reshape(8, 16, DS)
-            send(osum.at[i], orecv.at[i], o_send.at[i], o_recv.at[i], sib)
+            send(osum.at[i], orecv.at[i], o_send, o_recv.at[i], sib)
             return
         _, zz = source(k)
-        arrived(orecv.at[i], o_send.at[i], o_recv.at[i], sib)
+        arrived(orecv.at[i], o_recv.at[i], sib)
         fsend[i] = (acc.reshape(8, 16, DS) + orecv[i].astype(F32)).astype(BF16)
-        for j, (dh, dz) in enumerate(tp_others):
+        for dh, dz in tp_others:
             send(
                 fsend.at[i, lax.rem(z + dz, NZ) * NY + lax.rem(h + dh, NH)],
                 frecv.at[h * NZ + z, zz],
-                f_send.at[i, j],
-                f_recv.at[h * NZ + z, zz],
+                f_send,
+                f_recv,
                 dev_t(dh, dz),
             )
 
@@ -491,9 +473,16 @@
     down(6)
     down(7)
 
-    late = len(sent) - 7
-    for copy in sent[:late]:
-        copy.wait_send()
+    left(xb.at[tp, pl.ds(0, 7)], a_send.at[0], y_other)
+    left(xb.at[tp, pl.ds(0, 8)], a_send.at[1], h_other)
+    left(xb.at[tp, ks], k_sem.at[0], h_other)
+    left(xb.at[pl.ds(0, 14), xs], x_send.at[0], sib)
+    left(xb.at[pl.ds(0, 14), ks], x_send.at[1], sib)
+    left(pg.at[pl.ds(0, 7)], g_send, x_next)
+    left(pu.at[pl.ds(0, 7)], u_send, x_next)
+    left(hid.at[pl.ds(0, 7)], h_send, x_next)
+    left(osum, o_send, sib)
+    arrived(frecv.at[pl.ds(0, 7)], f_recv, h_other)
     for k in range(4):
         zz = lax.rem(z + OFFSETS[k], NZ)
         total = fsend[k, z * NY + h].astype(F32)
@@ -501,9 +490,8 @@
             [xb[t_of(c, zz, b), z * NY + h].astype(F32) for b in range(2)], axis=0
         )
         total = total + res
-        for i, (dh, dz) in enumerate(tp_others):
+        for dh, dz in tp_others:
             src = lax.rem(h + dh, NH) * NZ + lax.rem(z + dz, NZ)
-            arrived(frecv.at[src, zz], f_send.at[0, i], f_recv.at[src, zz], dev_t(dh, dz))
             total = total + frecv[src, zz].astype(F32)
         rounded = total.astype(BF16)
         rows = pl.ds(pl.multiple_of(zz * 16, 16), 16)
@@ -519,17 +507,17 @@
     rowsum = jnp.sum(sq[...].T, axis=0, keepdims=True)
     csend[:, 0:64] = jnp.broadcast_to(rowsum, (8, 64))
     csend[:, 64:128] = jnp.zeros((8, 64), F32)
-    for i, (dx, dy) in enumerate(dp_others):
-        send(csend, crecv.at[mine], c_send.at[i], c_recv.at[mine], dev_d(dx, dy))
+    for dx, dy in dp_others:
+        send(csend, crecv.at[mine], c_send, c_recv, dev_d(dx, dy))
+    left(frecv.at[pl.ds(0, 7)], f_send, h_other)
     total = csend[...]
-    for i, (dx, dy) in enumerate(dp_others):
+    arrived(crecv.at[pl.ds(0, 7)], c_recv, y_other)
+    for dx, dy in dp_others:
         g = lax.rem(x + dx, NX) * NY + lax.rem(y + dy, NY)
-        arrived(crecv.at[g], c_send.at[i], c_recv.at[g], dev_d(dx, dy))
         total = total + crecv[g]
     rc_ref[...] = total[0, 0:64] / D
     result.wait()
-    for copy in sent[late:]:
-        copy.wait_send()
+    left(crecv.at[pl.ds(0, 7)], c_send, y_other)
 
 
 def on_device(saved_input, keep_bits, norm_gain, gate_weight, up_weight, down_weight):
@@ -575,23 +563,24 @@
             pltpu.VMEM((8, 8, 128), F32),
             dma((3,)),
             dma((4,)),
-            dma((15,)),
-            dma((2, 8)),
             dma((2,)),
-            dma((2, 14)),
-            dma((2, 16)),
-            dma((8, 7)),
-            dma((8, 7)),
-            dma((8, 7)),
-            dma((8, 7)),
-            dma((8, 7)),
-            dma((8, 8)),
+            dma((2,)),
+            dma((2,)),
+            dma((2,)),
+            dma((16,)),
+            dma((5,)),
+            dma,
+            dma((8, 3)),
+            dma,
+            dma((8, 3)),
+            dma,
+            dma((8, 3)),
+            dma,
             dma((4,)),
-            dma((4,)),
-            dma((4, 7)),
-            dma((8, 4)),
-            dma((7,)),
-            dma((8,)),
+            dma,
+            dma,
+            dma,
+            dma,
         ],
         compiler_params=pltpu.CompilerParams(
             collective_id=0, has_side_effects=True, vmem_limit_bytes=56 * 1024 * 1024

time: 83.1 us -> 80.8 us (0.972)
  Pallas kernels: 79.5 us -> 77.3 us
    pallas_call x1, Pallas kernels: 79.5 us -> 77.3 us  [on_device(): pl.pallas_call(kernel, out_shape=(jax.ShapeDtypeStruct((64, DS), BF16), j...]
where the time goes in v5:
time: 80.8 us; the launch traced here: 80.7 us
  Pallas kernels  77.3 us (96%)
  local copies, waits for them, and re-layouts  2.74 us (3%)
    pallas_call x1, Pallas kernels, on_device(): pl.pallas_call(kernel, out_shape=(jax.ShapeDtypeStruct((64, DS), BF16), j...  77.3 us
    unnamed x2, local copies, waits for them, and re-layouts  2.74 us

profile of v5, /device:TPU:1, one launch (start us, length us, event | category | flops | bytes accessed | tf_op | source)
XLA Modules:
  0.0 80.7 jit_solution(8040925532567758247)
XLA Ops:
  0.6 77.3 %block.1 = (bf16[64,1024]{1,0:T(8,128)(2,1)}, f32[64]{0:T(128)}) custom-call(bf16[8,8192]{1,0:T(8,128)(2,1)} %x_hbm.1, s32[8,448]{1,0:T(8,128)} %kb_hbm.1, bf16[1024]{0:T(1024)(128)(2,1)} %gain_hbm.1, bf16[1024,896]{1,0:T(8,128)(2,1)} %wg_hbm.1, bf16[1024,896]{1,0:T(8,128)(2,1)} %wu_hbm.1, bf16[896,1024]{1,0:T(8,128)(2,1)} %wd_hbm.1), custom_call_target="tpu_custom_call" | custom-call | tf_op jit(solution)/shard_map/block/pallas_call | solution.py:527
  77.9 1.6 %copy.10 = bf16[64,1024]{1,0:T(8,128)(2,1)} copy(bf16[64,1024]{1,0:T(8,128)(2,1)} %get-tuple-element.4) | data formatting | bytes 262144
  79.5 1.2 %copy.11 = f32[64]{0:T(128)} copy(f32[64]{0:T(128)} %get-tuple-element.5) | data formatting | bytes 512

commit v6 on v5

--- a/solution.py
+++ b/solution.py
@@ -8,6 +8,7 @@
 D = 8192
 DS = 1024
 FU = 896
+FA, FB = 1024, 768
 MESH = pl.DeviceIdType.MESH
 F32 = jnp.float32
 BF16 = jnp.bfloat16
@@ -133,9 +134,12 @@
     row_others += [(dx, dy, 1) for dx, dy in [*dp_others, (0, 0)]]
 
     loads = [
-        pltpu.make_async_copy(wu_hbm, wu, w_sem.at[0]),
-        pltpu.make_async_copy(wg_hbm, wg, w_sem.at[1]),
+        pltpu.make_async_copy(wu_hbm.at[:, pl.ds(FA - FU, FB)], wu, w_sem.at[0]),
+        pltpu.make_async_copy(wg_hbm, wg.at[:, pl.ds(0, FU)], w_sem.at[1]),
         pltpu.make_async_copy(wd_hbm, wd, w_sem.at[2]),
+        pltpu.make_async_copy(
+            wu_hbm.at[:, pl.ds(0, FA - FU)], wg.at[:, pl.ds(FU, FA - FU)], w_sem.at[3]
+        ),
     ]
     rows_in = [
         pltpu.make_async_copy(x_hbm, x_ref, l_sem.at[0]),
@@ -279,6 +283,7 @@
         send(pu.at[k, 1 - y], u_y.at[k], u_send, u_done.at[k, 0], y_other)
         if k == 0:
             loads[1].wait()
+            loads[3].wait()
         acc = jnp.dot(lhs, wg[...], preferred_element_type=F32).astype(BF16)
         for g in range(8):
             pg[k, g // 2, g % 2] = acc[g * 16 : g * 16 + 16]
@@ -349,10 +354,11 @@
         bit = (byte.astype(jnp.int32) >> (unit & 7)) & 1
         keep = 2.0 * bit.astype(F32)
         arrived(yrecv.at[k], g_done.at[k, 2], y_other)
-        gate = (gate_over_x(k, y) + yrecv[k].astype(F32)) * inv
+        first = gate_over_x(k, y) + yrecv[k].astype(F32)
+        gate = first[:, :FU] * inv
         arrived(u_recv.at[k], u_done.at[k, 2], x_next)
         up = pu[k, y, x].astype(F32) + u_recv[k, 0].astype(F32) + u_recv[k, 1].astype(F32)
-        up = up.reshape(16, FU) * inv
+        up = jnp.concatenate((first[:, FU:], up.reshape(16, FB)), axis=1) * inv
         hid[k, x, y] = (gate / (1.0 + jnp.exp(-gate)) * up * keep).astype(BF16)
         near_y, far_y = 1 + y, 2 - y
         block = hid.at[k, x, y]
@@ -520,6 +526,28 @@
     left(crecv.at[pl.ds(0, 7)], c_send, y_other)
 
 
+def finish(out_ref, check_ref, out_hbm, check_hbm, rows, check, sems):
+    def copies(into):
+        j = 0 if into else 1
+        moves = []
+        for i in range(4):
+            held, cells = rows.at[i], pl.ds(i * 16, 16)
+            src, dst = (out_ref.at[cells], held) if into else (held, out_hbm.at[cells])
+            moves.append(pltpu.make_async_copy(src, dst, sems.at[j, i]))
+        src, dst = (check_ref, check) if into else (check, check_hbm)
+        moves.append(pltpu.make_async_copy(src, dst, sems.at[j, 4]))
+        return moves
+
+    taken, put = copies(True), copies(False)
+    for move in taken:
+        move.start()
+    for first, second in zip(taken, put):
+        first.wait()
+        second.start()
+    for move in put:
+        move.wait()
+
+
 def on_device(saved_input, keep_bits, norm_gain, gate_weight, up_weight, down_weight):
     vmem = pl.BlockSpec(memory_space=pltpu.VMEM)
     hbm = pl.BlockSpec(memory_space=pltpu.HBM)
@@ -533,8 +561,8 @@
         in_specs=[hbm] * 6,
         out_specs=(hbm, vmem),
         scratch_shapes=[
-            pltpu.VMEM((DS, FU), BF16),
-            pltpu.VMEM((DS, FU), BF16),
+            pltpu.VMEM((DS, FA), BF16),
+            pltpu.VMEM((DS, FB), BF16),
             pltpu.VMEM((FU, DS), BF16),
             pltpu.VMEM((128, FU), BF16),
             pltpu.VMEM((8, 512), jnp.int32),
@@ -543,15 +571,15 @@
             pltpu.VMEM((8, D), BF16),
             pltpu.VMEM((16, 10, 8, DS), BF16),
             pltpu.VMEM((128, DS), F32),
-            pltpu.VMEM((8, 4, 2, 16, FU), BF16),
-            pltpu.VMEM((8, 2, 4, 2, 8, FU), BF16),
-            pltpu.VMEM((8, 2, 16, FU), BF16),
-            pltpu.VMEM((8, 2, 2, 16, FU), BF16),
-            pltpu.VMEM((8, 2, 8, FU), BF16),
-            pltpu.VMEM((8, 2, 2, 8, FU), BF16),
-            pltpu.VMEM((8, 4, 2, 8, FU), BF16),
-            pltpu.VMEM((8, 16, FU), BF16),
-            pltpu.VMEM((8, 16, FU), BF16),
+            pltpu.VMEM((8, 4, 2, 16, FA), BF16),
+            pltpu.VMEM((8, 2, 4, 2, 8, FB), BF16),
+            pltpu.VMEM((8, 2, 16, FA), BF16),
+            pltpu.VMEM((8, 2, 2, 16, FA), BF16),
+            pltpu.VMEM((8, 2, 8, FB), BF16),
+            pltpu.VMEM((8, 2, 2, 8, FB), BF16),
+            pltpu.VMEM((8, 4, 2, 8, FB), BF16),
+            pltpu.VMEM((8, 16, FA), BF16),
+            pltpu.VMEM((8, 16, FA), BF16),
             pltpu.VMEM((8, 4, 2, 16, FU), BF16),
             pltpu.VMEM((4, 8, 16, DS), BF16),
             pltpu.VMEM((4, 8, 16, DS), BF16),
@@ -561,7 +589,7 @@
             pltpu.VMEM((64, 128), F32),
             pltpu.VMEM((8, 128), F32),
             pltpu.VMEM((8, 8, 128), F32),
-            dma((3,)),
+            dma((4,)),
             dma((4,)),
             dma((2,)),
             dma((2,)),
@@ -587,7 +615,21 @@
         ),
         name="block",
     )(saved_input, keep_bits, norm_gain, gate_weight, up_weight, down_weight)
-    return out, check
+    return pl.pallas_call(
+        finish,
+        out_shape=(
+            jax.ShapeDtypeStruct((64, DS), BF16),
+            jax.ShapeDtypeStruct((64,), F32),
+        ),
+        in_specs=[hbm, hbm],
+        out_specs=(hbm, hbm),
+        scratch_shapes=[
+            pltpu.VMEM((4, 16, DS), BF16),
+            pltpu.VMEM((64,), F32),
+            dma((2, 5)),
+        ],
+        name="finish",
+    )(out, check)
 
 
 def solution(mesh):

time: 80.8 us -> 78.7 us (0.974)
  local copies, waits for them, and re-layouts: 2.74 us -> 0 us
    unnamed x2 -> x0, local copies, waits for them, and re-layouts: 2.74 us -> none
    pallas_call x0 -> x1, Pallas kernels: none -> 1.51 us  [on_device(): pl.pallas_call(finish, out_shape=(jax.ShapeDtypeStruct((64, DS), BF16), j...]
    pallas_call x1, Pallas kernels: 77.3 us -> 76.3 us  [on_device(): pl.pallas_call(kernel, out_shape=(jax.ShapeDtypeStruct((64, DS), BF16), j...]
where the time goes in v6:
time: 78.7 us; the launch traced here: 78.4 us
  Pallas kernels  77.8 us (99%)
    pallas_call x1, Pallas kernels, on_device(): pl.pallas_call(kernel, out_shape=(jax.ShapeDtypeStruct((64, DS), BF16), j...  76.3 us

profile of v6, /device:TPU:1, one launch (start us, length us, event | category | flops | bytes accessed | tf_op | source)
XLA Modules:
  0.0 78.4 jit_solution(2306149666672972098)
XLA Ops:
  0.6 76.3 %block.1 = (bf16[64,1024]{1,0:T(8,128)(2,1)}, f32[64]{0:T(128)}) custom-call(bf16[8,8192]{1,0:T(8,128)(2,1)} %x_hbm.1, s32[8,448]{1,0:T(8,128)} %kb_hbm.1, bf16[1024]{0:T(1024)(128)(2,1)} %gain_hbm.1, bf16[1024,896]{1,0:T(8,128)(2,1)} %wg_hbm.1, bf16[1024,896]{1,0:T(8,128)(2,1)} %wu_hbm.1, bf16[896,1024]{1,0:T(8,128)(2,1)} %wd_hbm.1), custom_call_target="tpu_custom_call" | custom-call | tf_op jit(solution)/shard_map/block/pallas_call | solution.py:555
  76.9 1.5 %finish.1 = (bf16[64,1024]{1,0:T(8,128)(2,1)}, f32[64]{0:T(128)}) custom-call(bf16[64,1024]{1,0:T(8,128)(2,1)} %get-tuple-element.4.out_ref, f32[64]{0:T(128)} %get-tuple-element.5.check_ref), custom_call_target="tpu_custom_call" | custom-call | tf_op jit(solution)/shard_map/finish/pallas_call | solution.py:618
